TPU v7x, 256 devices: a 4x2x16 block of a 4x16x16 slice. The times are simulated.
256 devices in a mesh: groups: 2 (over y), chan: 64 (over x, z), sub: 2 (over core).
Axes of the slice: x: 4, y: 2, z: 16, core: 2. Of those that a mesh axis runs over, the one named last changes fastest.
The devices are a block of a 4x16x16 slice.
Arguments:
- predicted_sky_response: bfloat16 [131072, 8, 2, 128], P(('groups', 'chan', 'sub')), parts along dimension 0, may hold values from -0.4375 to 0.4375
- measured_correlation: bfloat16 [131072, 2, 128], P(('groups', 'chan', 'sub')), parts along dimension 0, may hold values from -6 to 6
- keep_indicator: int32 [131072, 128], P(('groups', 'chan', 'sub')), parts along dimension 0, may hold values 0 or 1
- tile_owner: int32 [131072, 1], P(('groups', 'chan', 'sub')), parts along dimension 0, may hold values from 0 to 63; in each aligned block of 512 rows (0 to 511, 512 to 1023, ...) at most 24 rows name the same one
- tile_channel: int32 [131072], P(('groups', 'chan', 'sub')), parts along dimension 0, may hold values from 0 to 3
- tile_base: int32 [131072], P(('groups', 'chan', 'sub')), parts along dimension 0, may hold values from 0 to 14
- pairs: int32 [15, 2, 128], replicated, may hold values from 0 to 61, as said below
- gains: float32 [512, 2, 62, 8], P(('groups', 'chan')), parts along dimension 0, may hold values from -5 to 5
- duals: float32 [512, 2, 62, 8], P(('groups', 'chan', 'sub')), parts along dimension 0, may hold values from -4 to 4
- consensus: float32 [8, 2, 62, 8], P('groups'), parts along dimension 0, may hold values from -5 to 5
- rho: float32 [8], replicated, may hold values from 0.3 to 3
Outputs:
- gains_new: float32 [512, 2, 62, 8], P(('groups', 'chan', 'sub')), parts along dimension 0
- consensus_new: float32 [8, 2, 62, 8], P('groups'), parts along dimension 0
- duals_new: float32 [512, 2, 62, 8], P(('groups', 'chan', 'sub')), parts along dimension 0
There are 2 independent parts, one for each index of `groups`. A program takes and returns all parts, laid end to end along the dimension named above; an argument that names none is the same for every part. Nothing has to cross between parts.
Inputs may be any that keep to these rules, and one draw needn't show every extreme that they name: `tile_owner`: on the tiles of one device at most 24 name the same owner, a bound that some block reaches. `pairs`: the two stations of a row differ.
All inputs are finite; a program needn't handle non-finite values. No bound on the sum of `keep_indicator` on one device may be relied on, other than what follows from the above.
Results may differ from a plain program's by a relative error of at most 0.0027.
Values may be sent and summed in bfloat16 or wider, within the bound.
A program may use at most 128 MiB of HBM per device.

v0:
```python
import functools
import math

import jax
import jax.numpy as jnp
from jax import lax
from jax.sharding import Mesh
from jax.sharding import PartitionSpec as P

CHAN = ("chan_0", "chan_1")
CHAN_SUB = ("chan_0", "chan_1", "sub")
GROUPS_CHAN_SUB = ("groups", "chan_0", "chan_1", "sub")
GROUPS_CHAN = ("groups", "chan_0", "chan_1")


def joined_along(pieces, dim):
    pieces = jnp.moveaxis(pieces, 0, dim)
    shape = pieces.shape
    return pieces.reshape(*shape[:dim], shape[dim] * shape[dim + 1], *shape[dim + 2 :])


def stacked_from(array, axes, sequence):
    pieces = array
    for k in sequence:
        pieces = lax.all_gather(pieces, axes[k])
    done = sequence[::-1]
    back = [done.index(k) for k in range(len(axes))]
    pieces = pieces.transpose(*back, *range(len(axes), pieces.ndim))
    return pieces.reshape(-1, *array.shape)


def gathered_by_axis(array, axes, sequence, dim):
    return joined_along(stacked_from(array, axes, sequence), dim)


def split_up(array, dim, count):
    before, after = (array.shape[:dim], array.shape[dim + 1 :])
    return jnp.moveaxis(array.reshape(*before, count, -1, *after), dim, 0)


def one_scatter(arrays, axis, dims):
    count = lax.axis_size(axis)
    pieces = [split_up(a, dim, count) for a, dim in zip(arrays, dims)]
    lines = jnp.concatenate([b.reshape(count, -1) for b in pieces], axis=1)
    rows = max(16, -(-lines.shape[1] // 1024) * 8)
    lines = jnp.pad(lines, ((0, 0), (0, rows * 128 - lines.shape[1]))).reshape(-1, 128)
    line, at, finished = (lax.psum_scatter(lines, axis, tiled=True).reshape(-1), 0, [])
    for b in pieces:
        part = b[0]
        finished.append(line[at : at + part.size].reshape(part.shape))
        at += part.size
    return tuple(finished)


def by_axis(array, axes):
    return functools.reduce(lax.psum, axes, array)


def legendre_rows(channels):
    positions = jnp.arange(channels, dtype=jnp.float32)
    abscissa = (2.0 * positions - (channels - 1)) / max(channels - 1, 1)
    return jnp.stack(
        [
            jnp.ones_like(abscissa),
            abscissa,
            0.5 * (3.0 * abscissa * abscissa - 1.0),
            0.5 * (5.0 * abscissa * abscissa * abscissa - 3.0 * abscissa),
        ]
    )


def outer_terms(vector_real, vector_imag, weight_real, weight_imag):
    tiles_count, row_total_count, directions = vector_real.shape
    outer_real = (
        vector_real[..., :, None] * vector_real[..., None, :]
        + vector_imag[..., :, None] * vector_imag[..., None, :]
    )
    outer_imag = (
        vector_real[..., :, None] * vector_imag[..., None, :]
        - vector_imag[..., :, None] * vector_real[..., None, :]
    )
    normal = jnp.stack([outer_real, outer_imag], axis=2).reshape(
        tiles_count, row_total_count, 2 * directions * directions
    )
    side_real = vector_real * weight_real[..., None] + vector_imag * weight_imag[..., None]
    side_imag = vector_real * weight_imag[..., None] - vector_imag * weight_real[..., None]
    right_side = jnp.stack([side_real, side_imag], axis=2).reshape(
        tiles_count, row_total_count, 2 * directions
    )
    return (normal, right_side)


def row_terms(coupling, observed, near_gain, far_gain):
    coupling_real = jnp.swapaxes(coupling[:, :, 0, :], 1, 2).astype(jnp.float32)
    coupling_imag = jnp.swapaxes(coupling[:, :, 1, :], 1, 2).astype(jnp.float32)
    near_real, near_imag = (near_gain[:, :, 0, :], near_gain[:, :, 1, :])
    far_real, far_imag = (far_gain[:, :, 0, :], far_gain[:, :, 1, :])
    slope_real = coupling_real * far_real + coupling_imag * far_imag
    slope_imag = coupling_imag * far_real - coupling_real * far_imag
    mirror_real = coupling_real * near_real - coupling_imag * near_imag
    mirror_imag = -(coupling_real * near_imag + coupling_imag * near_real)
    model_real = jnp.sum(near_real * slope_real - near_imag * slope_imag, axis=-1)
    model_imag = jnp.sum(near_real * slope_imag + near_imag * slope_real, axis=-1)
    observed_f = observed.astype(jnp.float32)
    residual_real = observed_f[:, 0, :] - model_real
    residual_imag = observed_f[:, 1, :] - model_imag
    normal_near, right_near = outer_terms(slope_real, slope_imag, residual_real, residual_imag)
    normal_far, right_far = outer_terms(mirror_real, mirror_imag, residual_real, -residual_imag)
    normal = jnp.concatenate([normal_near, normal_far], axis=1).astype(jnp.bfloat16)
    right_side = jnp.concatenate([right_near, right_far], axis=1).astype(jnp.bfloat16)
    return (normal, right_side)


def tile_normals(coupling, observed, channel_index, base_index, pairs, gain_table):
    stations_count = gain_table.shape[2]
    stations = pairs[base_index]
    station_ids = jnp.arange(stations_count, dtype=jnp.int32)
    near_onehot = (stations[:, 0, :, None] == station_ids).astype(jnp.float32)
    far_onehot = (stations[:, 1, :, None] == station_ids).astype(jnp.float32)
    tile_gains = gain_table[channel_index]
    near_gain = jnp.einsum(
        "trs,tcsk->trck", near_onehot, tile_gains, precision=lax.Precision.HIGHEST
    )
    far_gain = jnp.einsum("trs,tcsk->trck", far_onehot, tile_gains, precision=lax.Precision.HIGHEST)
    normal, right_side = row_terms(coupling, observed, near_gain, far_gain)
    both_onehot = jnp.concatenate([near_onehot, far_onehot], axis=1).astype(jnp.bfloat16)
    tile_normal = jnp.einsum(
        "trs,trc->tsc", both_onehot, normal, preferred_element_type=jnp.float32
    )
    tile_right = jnp.einsum(
        "trs,trc->tsc", both_onehot, right_side, preferred_element_type=jnp.float32
    )
    return (tile_normal, tile_right)


def accumulate(coupling, observed, channel_index, base_index, pairs, gain_table, channel_slots):
    tiles_count = coupling.shape[0]
    block_size = math.gcd(tiles_count, 32)
    iteration_tally = tiles_count // block_size
    stations_count = gain_table.shape[2]
    directions = gain_table.shape[3]

    def one_step(totals, block_item):
        normal_acc, right_acc = totals
        tile_normal, tile_right = tile_normals(
            block_item[0], block_item[1], block_item[2], block_item[3], pairs, gain_table
        )
        return (
            (
                normal_acc.at[block_item[2]].add(tile_normal),
                right_acc.at[block_item[2]].add(tile_right),
            ),
            None,
        )

    block_items = (
        coupling.reshape((iteration_tally, block_size) + coupling.shape[1:]),
        observed.reshape((iteration_tally, block_size) + observed.shape[1:]),
        channel_index.reshape(iteration_tally, block_size),
        base_index.reshape(iteration_tally, block_size),
    )
    start_totals = (
        jnp.zeros((channel_slots, stations_count, 2 * directions * directions), jnp.float32),
        jnp.zeros((channel_slots, stations_count, 2 * directions), jnp.float32),
    )
    (normal_sum, right_sum), _ = lax.scan(one_step, start_totals, block_items)
    return (normal_sum, right_sum)


def admm_update(normal, right_side, gain, dual, anchor, rho):
    count, stations = (normal.shape[0], normal.shape[1])
    directions = rho.shape[0]
    normal_blocks = normal.reshape(count, stations, 2, directions, directions)
    ridge_diag = jnp.diag(rho)
    higher_half_records = jnp.concatenate(
        [normal_blocks[:, :, 0] + ridge_diag, -normal_blocks[:, :, 1]], axis=-1
    )
    lower_rows = jnp.concatenate(
        [normal_blocks[:, :, 1], normal_blocks[:, :, 0] + ridge_diag], axis=-1
    )
    system = jnp.concatenate([higher_half_records, lower_rows], axis=-2)
    gain_rows = jnp.transpose(gain, (0, 2, 1, 3))
    dual_rows = jnp.transpose(dual, (0, 2, 1, 3))
    anchor_rows = jnp.transpose(anchor, (0, 2, 1, 3))
    target = (
        right_side.reshape(count, stations, 2, directions)
        - dual_rows
        - rho * (gain_rows - anchor_rows)
    )
    factor = jnp.linalg.cholesky(system)
    gain_step = jax.scipy.linalg.cho_solve(
        (factor, True), target.reshape(count, stations, 2 * directions)[..., None]
    )[..., 0]
    return gain + jnp.transpose(gain_step.reshape(count, stations, 2, directions), (0, 2, 1, 3))


def fit_consensus(poly_basis, summed):
    gram_matrix = jnp.dot(poly_basis, poly_basis.T, precision=lax.Precision.HIGHEST)
    factor = jnp.linalg.cholesky(gram_matrix)
    coeffs = jax.scipy.linalg.cho_solve((factor, True), summed.reshape(summed.shape[0], -1))
    return coeffs.reshape(summed.shape)


def body(
    predicted_sky_response,
    measured_correlation,
    keep_indicator,
    tile_owner,
    tile_channel,
    tile_base,
    pairs,
    gains,
    duals,
    consensus,
    rho,
):
    channels_here = gains.shape[0]
    chan_count = lax.axis_size(CHAN)
    sub_count = lax.axis_size("sub")
    half_count = channels_here // sub_count
    retained_selector = keep_indicator > 0
    predicted_response_kept = jnp.where(
        retained_selector[:, None, None, :],
        predicted_sky_response,
        jnp.zeros_like(predicted_sky_response),
    )
    measured_correlation_kept = jnp.where(
        retained_selector[:, None, :], measured_correlation, jnp.zeros_like(measured_correlation)
    )
    owner_index = tile_owner[:, 0]
    all_gains = gathered_by_axis(gains, CHAN, (0, 1), 0)
    full_channel = owner_index * channels_here + tile_channel
    normal_sum, right_sum = accumulate(
        predicted_response_kept,
        measured_correlation_kept,
        full_channel,
        tile_base,
        pairs,
        all_gains,
        channels_here * chan_count,
    )
    normal_part, right_part = one_scatter((normal_sum, right_sum), CHAN_SUB, (0, 0))
    sub_index = lax.axis_index("sub")
    chan_index = lax.axis_index(CHAN)
    my_gains = lax.dynamic_slice_in_dim(gains, sub_index * half_count, half_count, 0)
    poly_basis = legendre_rows(channels_here * chan_count)
    first_channel = (chan_index * sub_count + sub_index) * half_count
    my_basis = lax.dynamic_slice_in_dim(poly_basis, first_channel, half_count, 1)
    anchor = jnp.einsum("df,dcsk->fcsk", my_basis, consensus, precision=lax.Precision.HIGHEST)
    gains_new = admm_update(normal_part, right_part, my_gains, duals, anchor, rho)
    partial_value = jnp.einsum(
        "df,fcsk->dcsk", my_basis, gains_new + duals / rho, precision=lax.Precision.HIGHEST
    )
    summed = by_axis(partial_value, CHAN_SUB)
    consensus_new = fit_consensus(poly_basis, summed)
    duals_new = duals + rho * (
        gains_new
        - jnp.einsum("df,dcsk->fcsk", my_basis, consensus_new, precision=lax.Precision.HIGHEST)
    )
    return (gains_new, consensus_new, duals_new)


def solution(mesh):
    torus = Mesh(
        mesh.devices.reshape(mesh.shape["groups"], 4, 16, mesh.shape["sub"]),
        ("groups", "chan_0", "chan_1", "sub"),
    )
    return jax.shard_map(
        body,
        mesh=torus,
        in_specs=(
            P(GROUPS_CHAN_SUB, None, None, None),
            P(GROUPS_CHAN_SUB, None, None),
            P(GROUPS_CHAN_SUB, None),
            P(GROUPS_CHAN_SUB, None),
            P(GROUPS_CHAN_SUB),
            P(GROUPS_CHAN_SUB),
            P(),
            P(GROUPS_CHAN, None, None, None),
            P(GROUPS_CHAN_SUB, None, None, None),
            P("groups", None, None, None),
            P(),
        ),
        out_specs=(
            P(GROUPS_CHAN_SUB, None, None, None),
            P("groups", None, None, None),
            P(GROUPS_CHAN_SUB, None, None, None),
        ),
        check_vma=False,
    )
```

profile of v0, /device:TPU:33, one launch (start us, length us, event | category | flops | bytes accessed | tf_op | source)
XLA Modules:
  0.0 1092.0 jit_solution(16488837428794862589)
XLA Ops:
  10.5 10.8 all-gather
  21.3 54.7 %all-gather.1 = f32[64,4,2,62,8]{3,4,2,1,0:T(8,128)S(1)} all-gather(f32[4,4,2,62,8]{3,4,2,1,0:T(8,128)S(1)} %bitcast.312), channel_id=3, replica_groups=mesh['groups'=2,'chan_0'=4,'chan_1'=16,'sub'=2] {'chan_1'}, dimensions={0}, use_global_device_ids=true | all-gather | bytes 1079296 | tf_op jit(solution)/shard_map/all_gather | solution.py:25
  85.4 418.0 %while.12 = (s32[]{:T(128)}, f32[256,62,128]{2,1,0:T(8,128)}, f32[256,62,16]{1,2,0:T(8,128)}, s32[16,32]{1,0:T(8,128)S(1)}, s32[16,32]{1,0:T(8,128)S(1)}, /*inde...) while((s32[]{:T(128)}, f32[256,62,128]{2,1,0:T(8,128)}, ...), condition=%wide.region_5.6_spmd, body=%wide.region_0.5_spmd.sunk | while | flops 259593408 | bytes 29465352 | solution.py:166
  151.6 4.8 scatter_fusion
  203.9 4.8 scatter_fusion
  230.0 4.8 scatter_fusion
  256.2 4.8 scatter_fusion
  334.5 4.8 scatter_fusion
  360.6 4.8 scatter_fusion
  386.7 4.8 scatter_fusion
  412.9 4.8 scatter_fusion
  439.0 4.8 scatter_fusion
  465.2 4.8 scatter_fusion
  503.4 6.5 copy.156
  509.9 6.1 reshape_reshape.17
  516.0 8.6 reshape_reshape.16
  524.7 7.7 select_maximum_fusion
  532.3 9.9 reshape.330
  544.9 259.9 %reduce-scatter.2.cloned.1.call-done = f32[144,128]{1,0:T(8,128)} async-done(((f32[18432,128]{1,0:T(8,128)}), f32[144,128]{1,0:T(8,128)}) %reduce-scatter.2.cloned.1.call-update) | async-done | bytes 73744 | tf_op jit(solution)/shard_map/reduce_scatter | solution.py:47
  806.8 181.8 %custom-call.21 = f32[2,62,16,16]{3,2,1,0:T(8,128)S(1)} custom-call(f32[2,62,16,16]{3,2,1,0:T(8,128)S(1)} %broadcast_multiply_fusion), custom_call_target="Cholesky" | custom-call | tf_op jit(solution)/shard_map/jit(cholesky)/cholesky | solution.py:190
  989.3 5.4 custom-call.22
  997.2 12.8 %psum.21 = f32[4,2,62,8]{2,0,3,1:T(4,128)S(1)} all-reduce(f32[4,2,62,8]{2,0,3,1:T(4,128)S(1)} %fusion.46), channel_id=1, replica_groups=mesh['groups'=2,'chan_0'=4,'chan_1'=16,'sub'=2] {'chan_0'}, use_global_device_ids=true, to_apply=%region_11.12 | all-reduce | flops 3968 | bytes 31744 | tf_op jit(solution)/shard_map/psum | solution.py:56
  1010.0 40.6 %psum.22 = f32[4,2,62,8]{2,0,3,1:T(4,128)S(1)} all-reduce(f32[4,2,62,8]{2,0,3,1:T(4,128)S(1)} %psum.21), channel_id=1, replica_groups=mesh['groups'=2,'chan_0'=4,'chan_1'=16,'sub'=2] {'chan_1'}, use_global_device_ids=true, to_apply=%region_12.13 | all-reduce | flops 3968 | bytes 31744 | tf_op jit(solution)/shard_map/psum | solution.py:56
  1051.2 31.9 %psum.23 = f32[2,62,8,4]{1,3,2,0:T(4,128)S(1)} all-reduce(f32[2,62,8,4]{1,3,2,0:T(4,128)S(1)} %copy.174), channel_id=1, replica_groups=mesh['groups'=2,'chan_0'=4,'chan_1'=16,'sub'=2] {'sub'}, use_global_device_ids=true, to_apply=%region_13.14 | all-reduce | flops 3968 | bytes 31744 | tf_op jit(solution)/shard_map/psum | solution.py:56
  (964 shorter events, 388.4 us)
Async XLA Ops:
  7.2 988.6 %copy-start = (f32[4,2,62,8]{2,3,1,0:T(8,128)S(1)}, f32[4,2,62,8]{2,3,1,0:T(8,128)}, u32[]{:S(2)}) copy-start(f32[4,2,62,8]{2,3,1,0:T(8,128)} %param.22) | copy-start | bytes 47620
  7.2 797.6 %reduce-scatter.2.cloned.1.call-start = ((), (), s32[]{:S(2)}) async-start(), calls=%async_computation.1 | async-start | bytes 9510912 | tf_op jit(solution)/shard_map/reduce_scatter | solution.py:47
  85.4 4.3 copy-start.9
  111.5 4.3 copy-start.9
  137.6 4.3 copy-start.9
  159.6 4.1 copy-start.8
  159.6 4.1 copy-start.10
  159.6 4.1 copy-start.16
  163.8 4.3 copy-start.9
  189.9 4.3 copy-start.9
  216.0 4.3 copy-start.9
  242.1 4.3 copy-start.9
  268.2 4.3 copy-start.9
  294.3 4.3 copy-start.9
  316.3 4.1 copy-start.8
  316.3 4.1 copy-start.10
  320.5 4.3 copy-start.9
  346.6 4.3 copy-start.9
  372.7 4.3 copy-start.9
  398.9 4.3 copy-start.9
  425.0 4.3 copy-start.9
  451.2 4.3 copy-start.9
  477.3 4.3 copy-start.9
  806.7 189.1 %copy-start.20 = (f32[2,2,62,8]{2,3,1,0:T(8,128)S(1)}, f32[2,2,62,8]{2,3,1,0:T(8,128)}, u32[]{:S(2)}) copy-start(f32[2,2,62,8]{2,3,1,0:T(8,128)} %param.21) | copy-start | bytes 23812
  (208 other events, 403.2 us)
Sparse Core Ops, SparseCore 0:
  542.4 262.2 reduce-scatter.1
where the time goes:
time: 1100 us; the launch traced here: 1090 us
  other arithmetic  433 us (39%)
  waiting for transfers between devices  260 us (24%)
  local copies, waits for them, and re-layouts  153 us (14%)
  blocking collectives  151 us (14%)
  matrix products  76.2 us (7%)
  between operations  14.4 us (1%)
    reduce_scatter x1, waiting for transfers between devices, one_scatter(): lax.psum_scatter(lines, axis, tiled=True).reshape(-1)  260 us
    another operation x4, other arithmetic, admm_update(): factor = jnp.linalg.cholesky(system)  182 us
    psum x3, blocking collectives, by_axis(): return functools.reduce(lax.psum, axes, array)  85.3 us
    scatter-add x16, other arithmetic, one_step(): normal_acc.at[block_item[2]].add(tile_normal)  76.7 us
    all_gather x2, blocking collectives, stacked_from(): pieces = lax.all_gather(pieces, axes[k])  65.5 us
    scatter-add x16, other arithmetic, one_step(): right_acc.at[block_item[2]].add(tile_right)  64.6 us
    reshape x32, local copies, waits for them, and re-layouts, outer_terms(): jnp.stack([outer_real, outer_imag], axis=2)  42.5 us
    dot_general x16, matrix products, tile_normals(): jnp.einsum('trs,trc->tsc', both_onehot, normal, preferred_element_type=jn...  31.7 us
  transfers between devices with their start and end apart: 1, of which 1 were waited for; matrix products, arithmetic and copies ran while one was open for 0% of the time, Pallas kernels for 0%

commit v1 on v0

v1 whole, which is shorter than its diff:
```python
import functools
import math

import jax
import jax.numpy as jnp
import numpy as np
from jax import lax
from jax.experimental import pallas as pl
from jax.experimental.pallas import tpu as pltpu
from jax.sharding import Mesh
from jax.sharding import PartitionSpec as P

GROUPS_CHAN_SUB = ("groups", "chan_0", "chan_1", "sub")
GROUPS_CHAN = ("groups", "chan_0", "chan_1")
BF, F32 = jnp.bfloat16, jnp.float32
GROUP = 8
HALF = 64


def term_rows(directions):
    real, imag = {}, {}
    for k in range(directions):
        for m in range(k, directions):
            real[k, m] = len(real)
    for k in range(directions):
        for m in range(k + 1, directions):
            imag[k, m] = len(real) + len(imag)
    return real, imag


def legendre_rows(channels):
    positions = jnp.arange(channels, dtype=jnp.float32)
    abscissa = (2.0 * positions - (channels - 1)) / max(channels - 1, 1)
    return jnp.stack(
        [
            jnp.ones_like(abscissa),
            abscissa,
            0.5 * (3.0 * abscissa * abscissa - 1.0),
            0.5 * (5.0 * abscissa * abscissa * abscissa - 3.0 * abscissa),
        ]
    )


def gram_inverse(channels):
    x = (2.0 * np.arange(channels, dtype=np.float64) - (channels - 1)) / max(channels - 1, 1)
    basis = np.stack([np.ones_like(x), x, 0.5 * (3 * x * x - 1), 0.5 * (5 * x * x * x - 3 * x)])
    return np.linalg.inv(basis @ basis.T)


def tile_order(tile_base, bases):
    tiles = tile_base.shape[0]
    slots = tiles + GROUP * bases
    here = jnp.arange(tiles, dtype=jnp.int32)
    same = (tile_base[:, None] == tile_base[None, :]) & (here[None, :] < here[:, None])
    rank = jnp.sum(same.astype(jnp.int32), axis=1)
    rows = jnp.arange(bases, dtype=jnp.int32)
    counts = jnp.sum((tile_base[None, :] == rows[:, None]).astype(jnp.int32), axis=1)
    padded = (counts + GROUP - 1) // GROUP * GROUP
    start = jnp.sum(jnp.where(rows[None, :] < tile_base[:, None], padded[None, :], 0), axis=1)
    place = start + rank
    slot = jnp.arange(slots, dtype=jnp.int32)
    order = jnp.sum(jnp.where(place[None, :] == slot[:, None], here[None, :] - tiles, 0), axis=1) + tiles
    return order.astype(jnp.int32), (jnp.sum(padded) // GROUP).reshape(1).astype(jnp.int32)


def tile_kernel(order, groups, gain_row, home_row, base, sky, seen, keep, pairs, table, out,
                onehot, sky_s, seen_s, keep_s, gain_s, near_far, terms, sums):
    tiles, coupled, rows = sky.shape
    directions = coupled // 2
    bases = pairs.shape[0]
    real, imag = term_rows(directions)
    n_terms = directions * directions + 2 * directions
    devices = out.shape[0] - 1

    station = lax.rem(lax.broadcasted_iota(jnp.int32, (2 * HALF, rows), 0), HALF)
    for b in range(bases):
        for side in range(2):
            onehot[b, :, side * rows:(side + 1) * rows] = jnp.where(
                station == pairs[b, side:side + 1, :], 1.0, 0.0).astype(BF)

    def clear(i, carry):
        out[i] = jnp.zeros((n_terms, 2 * HALF), F32)
        return carry
    lax.fori_loop(0, devices + 1, clear, 0)
    lane = lax.broadcasted_iota(jnp.int32, (1, 2 * HALF), 1)

    def one_group(g, carry):
        for t in range(GROUP):
            named = order[g * GROUP + t]
            tile = jnp.where(named < tiles, named, 0)
            sky_s[pl.ds(t, coupled, stride=GROUP), :] = sky[tile].astype(F32)
            seen_s[pl.ds(t, 2, stride=GROUP), :] = seen[tile].astype(F32)
            keep_s[pl.ds(t, 1), :] = keep[pl.ds(tile, 1), :]
            gain_s[pl.ds(t, coupled, stride=GROUP), :] = table[gain_row[tile]].astype(F32)
        chosen = onehot.at[base[order[g * GROUP]]]
        near_far[...] = jnp.dot(gain_s[...].astype(BF), chosen[...], preferred_element_type=F32)

        kept = keep_s[...] > 0

        def block(ref, i):
            return ref[i * GROUP:(i + 1) * GROUP, :]

        res_r = jnp.where(kept, block(seen_s, 0), 0.0)
        res_i = jnp.where(kept, block(seen_s, 1), 0.0)
        a_r, a_i, b_r, b_i = [], [], [], []
        mod_r = mod_i = None
        for k in range(directions):
            c_r = jnp.where(kept, block(sky_s, 2 * k), 0.0)
            c_i = jnp.where(kept, block(sky_s, 2 * k + 1), 0.0)
            p_r, p_i = (near_far[(2 * k + c) * GROUP:(2 * k + c + 1) * GROUP, :rows] for c in range(2))
            q_r, q_i = (near_far[(2 * k + c) * GROUP:(2 * k + c + 1) * GROUP, rows:] for c in range(2))
            x_r = c_r * q_r + c_i * q_i
            x_i = c_i * q_r - c_r * q_i
            a_r.append(x_r)
            a_i.append(x_i)
            b_r.append(c_r * p_r - c_i * p_i)
            b_i.append(-(c_r * p_i + c_i * p_r))
            m_r = p_r * x_r - p_i * x_i
            m_i = p_r * x_i + p_i * x_r
            mod_r = m_r if mod_r is None else mod_r + m_r
            mod_i = m_i if mod_i is None else mod_i + m_i
        res_r = res_r - mod_r
        res_i = res_i - mod_i

        for side, (v_r, v_i, w_r, w_i) in enumerate(
                ((a_r, a_i, res_r, res_i), (b_r, b_i, res_r, -res_i))):
            made = [None] * n_terms
            pending = {}

            def put(j, value):
                pending[j] = value
                lo = j - j % 2
                if lo in pending and lo + 1 in pending:
                    both = jnp.concatenate([pending.pop(lo), pending.pop(lo + 1)], axis=0)
                    terms[lo * GROUP:(lo + 2) * GROUP, side * rows:(side + 1) * rows] = both.astype(BF)

            for (k, m), j in real.items():
                put(j, v_r[k] * v_r[m] + v_i[k] * v_i[m])
            for (k, m), j in imag.items():
                put(j, v_r[k] * v_i[m] - v_i[k] * v_r[m])
            first = directions * directions
            for k in range(directions):
                put(first + k, v_r[k] * w_r + v_i[k] * w_i)
            for k in range(directions):
                put(first + directions + k, v_r[k] * w_i - v_i[k] * w_r)

        sums[...] = lax.dot_general(terms[...], chosen[...], (((1,), (1,)), ((), ())),
                                    preferred_element_type=F32)
        for t in range(GROUP):
            named = order[g * GROUP + t]
            tile = jnp.where(named < tiles, named, 0)
            home = home_row[tile]
            row = jnp.where(named < tiles, lax.shift_right_logical(home, 1), devices)
            part = jnp.where(lane // HALF == jnp.bitwise_and(home, 1),
                             sums[pl.ds(t, n_terms, stride=GROUP), :], 0.0)
            out[row] = out[row] + part
        return carry

    lax.fori_loop(0, groups[0], one_group, 0)


def tile_sums(sky, seen, keep, order, groups, gain_row, home_row, base, pairs, table, devices):
    tiles, directions, _, rows = sky.shape
    n_terms = directions * directions + 2 * directions
    bases = pairs.shape[0]
    smem = pl.BlockSpec(memory_space=pltpu.SMEM)
    vmem = pl.BlockSpec(memory_space=pltpu.VMEM)
    coupled = 2 * directions
    return pl.pallas_call(
        tile_kernel,
        out_shape=jax.ShapeDtypeStruct((devices + 1, n_terms, 2 * HALF), F32),
        in_specs=[smem] * 5 + [vmem] * 5,
        out_specs=vmem,
        scratch_shapes=[
            pltpu.VMEM((bases, 2 * HALF, 2 * rows), BF),
            pltpu.VMEM((coupled * GROUP, rows), F32),
            pltpu.VMEM((2 * GROUP, rows), F32),
            pltpu.VMEM((GROUP, rows), jnp.int32),
            pltpu.VMEM((coupled * GROUP, 2 * HALF), F32),
            pltpu.VMEM((coupled * GROUP, 2 * rows), F32),
            pltpu.VMEM((n_terms * GROUP, 2 * rows), BF),
            pltpu.VMEM((n_terms * GROUP, 2 * HALF), F32),
        ],
        compiler_params=pltpu.CompilerParams(vmem_limit_bytes=40 * 1024 * 1024),
        name="tile_sums",
    )(order, groups, gain_row, home_row, base, sky.reshape(tiles, coupled, rows), seen, keep, pairs, table)


def eliminate(total, target, rho, full, directions):
    real, imag = term_rows(directions)
    lanes = total.shape[-1]
    for k in range(directions):
        for m in range(directions):
            re = real[min(k, m), max(k, m)]
            value = total[re:re + 1, :]
            if k == m:
                value = value + rho[k:k + 1, :]
                full[1, k * directions + m:k * directions + m + 1, :] = jnp.zeros((1, lanes), F32)
            else:
                im = imag[min(k, m), max(k, m)]
                imv = total[im:im + 1, :]
                full[1, k * directions + m:k * directions + m + 1, :] = imv if k < m else -imv
            full[0, k * directions + m:k * directions + m + 1, :] = value
    row_r = [full[0, k * directions:(k + 1) * directions, :] for k in range(directions)]
    row_i = [full[1, k * directions:(k + 1) * directions, :] for k in range(directions)]
    t_r = [target[k:k + 1, :] for k in range(directions)]
    t_i = [target[directions + k:directions + k + 1, :] for k in range(directions)]
    for k in range(directions):
        inv = 1.0 / row_r[k][k:k + 1, :]
        row_r[k] = row_r[k] * inv
        row_i[k] = row_i[k] * inv
        t_r[k] = t_r[k] * inv
        t_i[k] = t_i[k] * inv
        for m in range(directions):
            if m == k:
                continue
            f_r = row_r[m][k:k + 1, :]
            f_i = row_i[m][k:k + 1, :]
            row_r[m], row_i[m] = (row_r[m] - (f_r * row_r[k] - f_i * row_i[k]),
                                  row_i[m] - (f_r * row_i[k] + f_i * row_r[k]))
            t_r[m], t_i[m] = (t_r[m] - (f_r * t_r[k] - f_i * t_i[k]),
                              t_i[m] - (f_r * t_i[k] + f_i * t_r[k]))
    return jnp.concatenate(t_r + t_i, axis=0)


XS, ZS = "chan_0", "chan_1"


def place():
    return lax.axis_index(XS), lax.axis_index(ZS), lax.axis_index("sub")


def sender(src, dst, send_sem, recv_sem, x, z, s):
    return pltpu.make_async_remote_copy(
        src_ref=src, dst_ref=dst, send_sem=send_sem, recv_sem=recv_sem,
        device_id={XS: x, ZS: z, "sub": s}, device_id_type=pl.DeviceIdType.MESH)


def meet(x, z, s, nx, nz, crossed):
    barrier = pltpu.get_barrier_semaphore()

    def ring(d, carry):
        pl.semaphore_signal(barrier, inc=1, device_id={XS: x, ZS: lax.rem(z + d, nz), "sub": s},
                            device_id_type=pl.DeviceIdType.MESH)
        return carry
    lax.fori_loop(1, nz, ring, 0)
    near = [(e, f) for e in range(nx) for f in range(2) if e + f > 0 and (crossed or e * f == 0)]
    for e, f in near:
        pl.semaphore_signal(barrier, inc=1,
                            device_id={XS: lax.rem(x + e, nx), ZS: z, "sub": s + f - 2 * s * f},
                            device_id_type=pl.DeviceIdType.MESH)
    return barrier, nz - 1 + len(near)


def outward(i, nz):
    return jnp.where(lax.rem(i, 2) == 0, i // 2 + 1, nz - 1 - i // 2)


def gather_kernel(nx, nz, mine, table, z_recv, z_send, x_recv, x_send, c_recv, c_send):
    x, z, s = place()
    here, half = mine.shape[0], mine.shape[0] // 2
    barrier, count = meet(x, z, s, nx, nz, False)
    table[pl.ds((x * nz + z) * here + s * half, half)] = mine[pl.ds(s * half, half)]
    pl.semaphore_wait(barrier, count)

    def block(xx, zz):
        return table.at[pl.ds((xx * nz + zz) * here + s * half, half)]

    def rows(xx, h):
        return table.at[pl.ds(xx * nz * here, nz * here)].reshape(nz, here, *mine.shape[1:]).at[:, pl.ds(h * half, half)]

    own = mine.at[pl.ds(s * half, half)]

    def z_copy(d):
        return sender(own, block(x, z), z_send.at[d], z_recv.at[d], x, lax.rem(z + d, nz), s)

    def start_z(i, carry):
        z_copy(outward(i, nz)).start()
        return carry
    lax.fori_loop(0, nz - 1, start_z, 0)

    def x_copy(src, zz, d, e):
        return sender(src, block(x, zz), x_send.at[e, d], x_recv.at[e, d], lax.rem(x + e, nx), z, s)
    for e in range(1, nx):
        x_copy(own, z, 0, e).start()

    def pass_on(i, carry):
        d = outward(i, nz)
        zz = lax.rem(z + nz - d, nz)
        sender(own, block(x, zz), z_send.at[d], z_recv.at[d], x, z, s).wait_recv()
        for e in range(1, nx):
            x_copy(block(x, zz), zz, d, e).start()
        return carry
    lax.fori_loop(0, nz - 1, pass_on, 0)

    def c_copy(e, h):
        xx = lax.rem(x + nx - e, nx)
        return sender(rows(xx, h), rows(xx, h), c_send.at[e], c_recv.at[e], x, z, 1 - s)
    for e in (0, 1, 3, 2):
        if e > 0:
            xx = lax.rem(x + nx - e, nx)

            def arrived(d, carry):
                zz = lax.rem(z + nz - d, nz)
                sender(own, block(xx, zz), x_send.at[e, d], x_recv.at[e, d], x, z, s).wait_recv()
                return carry
            lax.fori_loop(0, nz, arrived, 0)
        c_copy(e, s).start()
    for e in range(nx):
        c_copy(e, 1 - s).wait_recv()

    def done_z(d, carry):
        z_copy(d).wait_send()
        return carry
    lax.fori_loop(1, nz, done_z, 0)
    for e in range(1, nx):
        def done_x(d, carry):
            x_copy(own, z, d, e).wait_send()
            return carry
        lax.fori_loop(0, nz, done_x, 0)
    for e in range(nx):
        c_copy(e, s).wait_send()


def gather_gains(mine, nx, nz):
    vmem = pl.BlockSpec(memory_space=pltpu.VMEM)
    dma = pltpu.SemaphoreType.DMA
    return pl.pallas_call(
        functools.partial(gather_kernel, nx, nz),
        out_shape=jax.ShapeDtypeStruct((nx * nz * mine.shape[0],) + mine.shape[1:], mine.dtype),
        in_specs=[vmem],
        out_specs=vmem,
        scratch_shapes=[dma((nz,)), dma((nz,)), dma((nx, nz)), dma((nx, nz)), dma((nx,)), dma((nx,))],
        compiler_params=pltpu.CompilerParams(collective_id=0, has_side_effects=True),
        name="gather_gains",
    )(mine)


def packed(v, plain):
    head = v[plain:].astype(BF)
    tail = v[plain:] - head.astype(F32)
    return jnp.concatenate([v[:plain].astype(BF), head, tail.astype(BF)], axis=0)


def unpacked(w, plain):
    v = w.astype(F32)
    mid = (v.shape[0] + plain) // 2
    return jnp.concatenate([v[:plain], v[plain:mid] + v[mid:]], axis=0)


def finish_kernel(nx, nz, inverse, sums, gain, dual, cons, basis, rho, gain_new, cons_new, dual_new,
                  peer, x_out, x_in, z_out, z_in, own_z, total, full, part_out, part_in, ring_in, last_in,
                  c_send, c_recv, x_send, x_recv, z_send, z_recv, p_send, p_recv, r_send, r_recv, l_send, l_recv):
    x, z, s = place()
    directions = rho.shape[0]
    degrees = basis.shape[0]
    plain = directions * directions
    chunk = 4
    nodes = nx * nz
    barrier, count = meet(x, z, s, nx, nz, True)
    pl.semaphore_wait(barrier, count)

    def far(i):
        step = (i + 1) // 2
        return lax.rem(jnp.where(lax.rem(i, 2) == 0, nz // 2 + step, nz // 2 + nz - step), nz)

    def c_copy(e, h):
        xx = lax.rem(x + e, nx)
        return sender(sums.at[pl.ds(h * nodes + xx * nz, nz)], peer.at[pl.ds(xx * nz, nz)],
                      c_send.at[e], c_recv.at[e], x, z, 1 - s)
    order = (2, 1, 3, 0)
    for e in order:
        c_copy(e, 1 - s).start()

    def pair_sum(xx, zz):
        return sums[s * nodes + xx * nz + zz] + peer[xx * nz + zz]

    def x_copy(e, c):
        at = pl.ds(c * chunk, chunk)
        return sender(x_out.at[e, at], x_in.at[e, at], x_send.at[e, c], x_recv.at[e, c],
                      lax.rem(x + e, nx), z, s)
    chunks = nz // chunk
    for e in order[:-1]:
        c_copy(e, s).wait_recv()
    c_copy(0, s).wait_recv()

    def fill_x(c, carry):
        for e in order[:-1]:
            def one(j, inner):
                i = c * chunk + j
                x_out[e, i] = packed(pair_sum(lax.rem(x + e, nx), lax.rem(z + far(i), nz)), plain)
                return inner
            lax.fori_loop(0, chunk, one, 0)
            x_copy(e, c).start()
        return carry
    lax.fori_loop(0, chunks, fill_x, 0)

    def z_copy(i):
        return sender(z_out.at[i], z_in.at[i], z_send.at[i], z_recv.at[i], x, lax.rem(z + far(i), nz), s)

    def fill_z(c, carry):
        for e in order[:-1]:
            x_copy(e, c).wait_recv()

        def one(j, inner):
            i = c * chunk + j
            acc = pair_sum(x, lax.rem(z + far(i), nz))
            for e in range(1, nx):
                acc = acc + unpacked(x_in[e, i], plain)
            z_out[i] = packed(acc, plain)
            own_z[...] = acc

            @pl.when(i < nz - 1)
            def _():
                z_copy(i).start()
            return inner
        lax.fori_loop(0, chunk, one, 0)
        return carry
    lax.fori_loop(0, chunks, fill_z, 0)
    total[...] = own_z[...]

    def take_z(i, carry):
        z_copy(i).wait_recv()
        total[...] = total[...] + unpacked(z_in[i], plain)
        return carry
    lax.fori_loop(0, nz - 1, take_z, 0)

    rho2 = jnp.concatenate([rho[...], rho[...]], axis=0)
    anchor = sum(basis[d:d + 1, :] * cons[d] for d in range(degrees))
    target = total[plain:, :] - dual[...] - rho2 * (gain[...] - anchor)
    new = gain[...] + eliminate(total, target, rho[...], full, directions)
    gain_new[...] = new
    weighted = new + dual[...] / rho2
    left = lax.broadcasted_iota(jnp.int32, (2 * directions, 2 * HALF), 1) < HALF

    def folded(d):
        part = basis[d:d + 1, :] * weighted
        return part + pltpu.roll(part, HALF, axis=1)
    pair = degrees // 2
    both = jnp.concatenate([jnp.where(left, folded(d), folded(d + pair)) for d in range(pair)], axis=0)
    pieces, piece = part_out.shape[0], part_out.shape[1]
    for m in range(pieces):
        part_out[m] = both[m * piece:(m + 1) * piece, :]

    near = [(e, f) for e in range(nx) for f in range(2) if e + f > 0]

    def other(e, f):
        return lax.rem(x + e, nx), s + f - 2 * s * f

    def p_copy(e, f):
        xx, ss = other(e, f)
        return sender(part_out.at[xx * 2 + ss], part_in.at[e * 2 + f], p_send.at[e * 2 + f],
                      p_recv.at[e * 2 + f], xx, z, ss)
    for e, f in near:
        p_copy(e, f).start()
    acc = part_out[x * 2 + s]
    for e, f in near:
        p_copy(e, f).wait_recv()
        acc = acc + part_in[e * 2 + f]
    ring_in[z] = acc

    def r_copy(d):
        zz = lax.rem(z + d, nz)
        return sender(ring_in.at[z], ring_in.at[z], r_send.at[d], r_recv.at[d], x, zz, s)

    def start_r(i, carry):
        r_copy(far(i)).start()
        return carry
    lax.fori_loop(0, nz - 1, start_r, 0)

    def take_r(i, carry):
        d = far(i)
        zz = lax.rem(z + nz - d, nz)
        sender(ring_in.at[zz], ring_in.at[zz], r_send.at[d], r_recv.at[d], x, z, s).wait_recv()
        return carry
    lax.fori_loop(0, nz - 1, take_r, 0)
    acc = ring_in[0]
    for i in range(1, nz):
        acc = acc + ring_in[i]
    me = x * 2 + s
    last_in[me] = acc

    def l_copy(e, f, m):
        xx, ss = other(e, f)
        return sender(last_in.at[m], last_in.at[m], l_send.at[e * 2 + f], l_recv.at[e * 2 + f], xx, z, ss)
    for e, f in near:
        l_copy(e, f, me).start()
    for e, f in near:
        back = lax.rem(x + nx - e, nx) * 2 + (s + f - 2 * s * f)
        l_copy(e, f, back).wait_recv()
    both = jnp.concatenate([last_in[m] for m in range(pieces)], axis=0)
    wide = 2 * directions
    summed = [None] * degrees
    for d in range(pair):
        rows = both[d * wide:(d + 1) * wide, :]
        turned = pltpu.roll(rows, HALF, axis=1)
        summed[d] = jnp.where(left, rows, turned)
        summed[d + pair] = jnp.where(left, turned, rows)
    fit = None
    for d in range(degrees):
        coeff = sum(inverse[d][q] * summed[q] for q in range(degrees))
        cons_new[d] = coeff
        term = basis[d:d + 1, :] * coeff
        fit = term if fit is None else fit + term
    dual_new[...] = dual[...] + rho2 * (new - fit)

    for e in range(nx):
        c_copy(e, 1 - s).wait_send()

    def sent_x(c, carry):
        for e in range(1, nx):
            x_copy(e, c).wait_send()
        return carry
    lax.fori_loop(0, chunks, sent_x, 0)

    def sent_z(i, carry):
        z_copy(i).wait_send()
        r_copy(i + 1).wait_send()
        return carry
    lax.fori_loop(0, nz - 1, sent_z, 0)
    for e, f in near:
        p_copy(e, f).wait_send()
        l_copy(e, f, me).wait_send()


def finish(sums, gain, dual, cons, basis, rho, inverse, nx, nz):
    vmem = pl.BlockSpec(memory_space=pltpu.VMEM)
    dma = pltpu.SemaphoreType.DMA
    degrees, directions = basis.shape[0], rho.shape[0]
    terms, lanes = sums.shape[1:]
    wire = terms + 2 * directions
    pieces = 2 * nx
    piece = degrees * 2 * directions // 2 // pieces
    chunks = nz // 4
    return pl.pallas_call(
        functools.partial(finish_kernel, nx, nz, inverse),
        out_shape=(jax.ShapeDtypeStruct(gain.shape, F32), jax.ShapeDtypeStruct(cons.shape, F32),
                   jax.ShapeDtypeStruct(gain.shape, F32)),
        in_specs=[vmem] * 6,
        out_specs=(vmem, vmem, vmem),
        scratch_shapes=[
            pltpu.VMEM((nx * nz, terms, lanes), F32),
            pltpu.VMEM((nx, nz, wire, lanes), BF),
            pltpu.VMEM((nx, nz, wire, lanes), BF),
            pltpu.VMEM((nz, wire, lanes), BF),
            pltpu.VMEM((nz, wire, lanes), BF),
            pltpu.VMEM((terms, lanes), F32),
            pltpu.VMEM((terms, lanes), F32),
            pltpu.VMEM((2, directions * directions, lanes), F32),
            pltpu.VMEM((pieces, piece, lanes), F32),
            pltpu.VMEM((pieces, piece, lanes), F32),
            pltpu.VMEM((nz, piece, lanes), F32),
            pltpu.VMEM((pieces, piece, lanes), F32),
            dma((nx,)), dma((nx,)), dma((nx, chunks)), dma((nx, chunks)), dma((nz,)), dma((nz,)),
            dma((pieces,)), dma((pieces,)), dma((nz,)), dma((nz,)), dma((pieces,)), dma((pieces,)),
        ],
        compiler_params=pltpu.CompilerParams(collective_id=1, has_side_effects=True,
                                             vmem_limit_bytes=40 * 1024 * 1024),
        name="finish",
    )(sums, gain, dual, cons, basis, rho)


def to_lanes(x):
    h, c, s, k = x.shape
    x = jnp.pad(x, ((0, 0), (0, 0), (0, HALF - s), (0, 0)))
    return jnp.transpose(x, (1, 3, 0, 2)).reshape(c * k, h * HALF)


def from_lanes(x, stations):
    rows, lanes = x.shape
    x = x.reshape(2, rows // 2, lanes // HALF, HALF)[..., :stations]
    return jnp.transpose(x, (2, 0, 3, 1))


def gain_table(gains):
    n, c, s, k = gains.shape
    x = jnp.pad(jnp.transpose(gains, (0, 3, 1, 2)).reshape(n, k * c, s), ((0, 0), (0, 0), (0, HALF - s)))
    head = lax.reduce_precision(x, 8, 7)
    return jnp.concatenate([head, x - head], axis=-1).astype(BF)


def body(sky, seen, keep, tile_owner, tile_channel, tile_base, pairs, gains, duals, consensus, rho):
    channels_here, _, stations, directions = gains.shape
    chan_count = lax.axis_size(("chan_0", "chan_1"))
    sub_count = lax.axis_size("sub")
    half_count = channels_here // sub_count
    devices = chan_count * sub_count
    sub_index = lax.axis_index("sub")
    chan_index = lax.axis_index(("chan_0", "chan_1"))

    nx, nz = lax.axis_size(XS), lax.axis_size(ZS)
    table = gather_gains(gain_table(gains), nx, nz)
    owner = tile_owner[:, 0]
    order, groups = tile_order(tile_base, pairs.shape[0])
    home = ((tile_channel // half_count) * chan_count + owner) * half_count + tile_channel % half_count
    sums = tile_sums(sky, seen, keep, order, groups, owner * channels_here + tile_channel, home,
                     tile_base, pairs, table, devices)

    my_gains = lax.dynamic_slice_in_dim(gains, sub_index * half_count, half_count, 0)
    channels = channels_here * chan_count
    first_channel = (chan_index * sub_count + sub_index) * half_count
    my_basis = lax.dynamic_slice_in_dim(legendre_rows(channels), first_channel, half_count, 1)
    basis = jnp.repeat(my_basis, HALF, axis=1)
    cons = jax.vmap(lambda c: to_lanes(jnp.stack([c, c])))(consensus)
    gain_l, dual_l = to_lanes(my_gains), to_lanes(duals)
    rho_l = jnp.broadcast_to(rho[:, None], (directions, 2 * HALF))
    new_l, fitted, dual_new = finish(sums, gain_l, dual_l, cons, basis, rho_l,
                                     gram_inverse(channels).tolist(), nx, nz)
    consensus_new = jax.vmap(lambda x: from_lanes(x, stations)[0])(fitted)
    return from_lanes(new_l, stations), consensus_new, from_lanes(dual_new, stations)


def solution(mesh):
    groups, subs = mesh.shape["groups"], mesh.shape["sub"]
    torus = Mesh(mesh.devices.reshape(groups, 4, mesh.shape["chan"] // 4, subs), GROUPS_CHAN_SUB)
    return jax.shard_map(
        body,
        mesh=torus,
        in_specs=(
            P(GROUPS_CHAN_SUB, None, None, None),
            P(GROUPS_CHAN_SUB, None, None),
            P(GROUPS_CHAN_SUB, None),
            P(GROUPS_CHAN_SUB, None),
            P(GROUPS_CHAN_SUB),
            P(GROUPS_CHAN_SUB),
            P(),
            P(GROUPS_CHAN, None, None, None),
            P(GROUPS_CHAN_SUB, None, None, None),
            P("groups", None, None, None),
            P(),
        ),
        out_specs=(
            P(GROUPS_CHAN_SUB, None, None, None),
            P("groups", None, None, None),
            P(GROUPS_CHAN_SUB, None, None, None),
        ),
        check_vma=False,
    )
```

time: 1100 us -> 155 us (0.14)
  other arithmetic: 433 us -> 3.58 us
  waiting for transfers between devices: 260 us -> 0 us
  blocking collectives: 151 us -> 0 us
  local copies, waits for them, and re-layouts: 153 us -> 11.1 us
  Pallas kernels: 0 us -> 137 us
  matrix products: 76.2 us -> 0 us
    reduce_scatter x1 -> x0, waiting for transfers between devices: 260 us -> none  [one_scatter(): lax.psum_scatter(lines, axis, tiled=True).reshape(-1)]
    another operation x108 -> x1, other arithmetic: 233 us -> 0.01 us  [the longest x4 182 us: admm_update(): factor = jnp.linalg.cholesky(system)]
    scatter-add x32 -> x0, other arithmetic: 141 us -> none  [the longest x16 76.7 us: one_step(): normal_acc.at[block_item[2]].add(tile_normal)]
    pallas_call x0 -> x3, Pallas kernels: none -> 137 us  [the longest x1 53.2 us: finish(): pl.pallas_call(functools.partial(finish_kernel, nx, nz, inverse), out_sha...]
    psum x3 -> x0, blocking collectives: 85.3 us -> none  [by_axis(): return functools.reduce(lax.psum, axes, array)]
    all_gather x2 -> x0, blocking collectives: 65.5 us -> none  [stacked_from(): pieces = lax.all_gather(pieces, axes[k])]
    dot_general x36 -> x0, matrix products: 55.1 us -> none  [the longest x16 31.7 us: tile_normals(): jnp.einsum('trs,trc->tsc', both_onehot, normal, preferred_element_type=jn...]
    reshape x36 -> x7, local copies, waits for them, and re-layouts: 53.4 us -> 0.6 us  [the longest x3 0.26 us: to_lanes(): return jnp.transpose(x, (1, 3, 0, 2)).reshape(c * k, h * HALF)]
  transfers between devices with their start and end apart: 1 -> 0, of which waited for: 1 -> 0; matrix products, arithmetic and copies ran while one was open for 0% -> 0% of each run, Pallas kernels for 0% -> 0%
where the time goes in v1:
time: 155 us
  Pallas kernels  137 us (88%)
  local copies, waits for them, and re-layouts  11.1 us (7%)
  other arithmetic  3.58 us (2%)
  between operations  3.47 us (2%)
    pallas_call x1, Pallas kernels, finish(): pl.pallas_call(functools.partial(finish_kernel, nx, nz, inverse), out_sha...  53.2 us
    pallas_call x1, Pallas kernels, gather_gains(): pl.pallas_call(functools.partial(gather_kernel, nx, nz), out_shape=jax.Sh...  46.6 us
    pallas_call x1, Pallas kernels, tile_sums(): pl.pallas_call(tile_kernel, out_shape=jax.ShapeDtypeStruct((devices + 1,...  37 us
    unnamed x31, local copies, waits for them, and re-layouts  8.89 us

profile of v1, /device:TPU:33, one launch (start us, length us, event | category | flops | bytes accessed | tf_op | source)
XLA Modules:
  0.0 154.9 jit_solution(1813697948234364529)
XLA Ops:
  0.7 0.9 convert_reduce_fusion.1
  1.6 0.6 fusion.15
  4.8 0.8 copy.21
  5.6 0.7 pad_maximum_fusion.mine
  6.3 46.6 %gather_gains.1.table = bf16[256,16,128]{2,1,0:T(8,128)(2,1)} custom-call(bf16[4,16,128]{2,1,0:T(8,128)(2,1)} %pad_maximum_fusion.mine), custom_call_target="tpu_custom_call" | custom-call | tf_op jit(solution)/shard_map/gather_gains/pallas_call | solution.py:328
  52.9 0.8 select_reduce_fusion.1
  53.7 0.2 convert_reduce_fusion
  54.0 0.2 select_reduce_fusion
  54.3 1.2 copy-done.2
  55.5 1.6 %copy-done.3 = bf16[512,8,2,128]{3,2,1,0:T(2,128)(2,1)S(1)} copy-done((bf16[512,8,2,128]{3,2,1,0:T(2,128)(2,1)S(1)}, bf16[512,8,2,128]{3,2,1,0:T(2,128)(2,1)}, u32[]{:S(2)}) %copy-start.3) | copy-done | bytes 2097176
  57.1 37.0 %tile_sums.1.sums = f32[129,80,128]{2,1,0:T(8,128)S(1)} custom-call(s32[632]{0:T(1024)S(1)} %broadcast_add_fusion.order, s32[1]{0:T(128)} %bitcast.groups, s32[512]{0:T(512)S(1)} %get-tuple-element.14.gain_row, s32[512]{0:T(512)S(1)} %get-tuple-element.13.home_row, s32[512]{0:T(512)S(1)} %copy-done.6, bf16[512,16,128]{2,1,0:T(8,128)(2,1)S(1)} %bitcast.27, ...), custom_call_target="tpu_custom_call" | custom-call | tf_op jit(solution)/shard_map/tile_sums/pallas_call | solution.py:169
  94.1 2.3 %copy-done = f32[129,80,128]{2,1,0:T(8,128)} copy-done((f32[129,80,128]{2,1,0:T(8,128)}, f32[129,80,128]{2,1,0:T(8,128)S(1)}, u32[]{:S(2)}) %copy-start) | copy-done | bytes 5283864
  96.6 0.1 reshape.116.basis
  96.7 0.1 reshape.113.gain
  96.9 0.1 reshape.115.cons
  97.0 0.1 reshape.114.dual
  97.1 2.5 %copy-done.1 = f32[129,80,128]{2,1,0:T(8,128)S(1)} copy-done((f32[129,80,128]{2,1,0:T(8,128)S(1)}, f32[129,80,128]{2,1,0:T(8,128)}, u32[]{:S(2)}) %copy-start.1) | copy-done | bytes 5283864
  99.6 53.2 %finish.1 = (f32[16,128]{1,0:T(8,128)S(1)}, f32[4,16,128]{2,1,0:T(8,128)S(1)}, f32[16,128]{1,0:T(8,128)S(1)}) custom-call(f32[129,80,128]{2,1,0:T(8,128)S(1)} %copy-done.1, f32[16,128]{1,0:T(8,128)S(1)} %reshape.113.gain, f32[16,128]{1,0:T(8,128)S(1)} %reshape.114.dual, f32[4,16,128]{2,1,0:T(8,128)S(1)} %reshape.115.cons, f32[4,128]{1,0:T(4,128)S(1)} %reshape.116.basis, ...), custom_call_target="tpu_custom_call" | custom-call | tf_op jit(solution)/shard_map/finish/pallas_call | solution.py:535
  152.8 0.1 reshape.118
  152.9 0.6 slice_bitcast_fusion
  153.6 0.1 reshape.119
  153.6 0.6 copy.35
  154.2 0.1 reshape.117
  154.3 0.6 copy.36
  (43 shorter events, 0.5 us)
Async XLA Ops:
  0.6 53.1 %copy-start.6 = (s32[512]{0:T(512)S(1)}, s32[512]{0:T(512)}, u32[]{:S(2)}) copy-start(s32[512]{0:T(512)} %base.1) | copy-start | bytes 6148
  0.6 53.6 %copy-start.11 = (s32[512,1]{0,1:T(1,128)S(1)}, s32[512,1]{0,1:T(1,128)}, u32[]{:S(2)}) copy-start(s32[512,1]{0,1:T(1,128)} %param.14) | copy-start | bytes 6148
  0.7 53.6 %copy-start.12 = (s32[512]{0:T(512)S(1)}, s32[512]{0:T(512)}, u32[]{:S(2)}) copy-start(s32[512]{0:T(512)} %param.15) | copy-start | bytes 6148
  0.7 53.6 %copy-start.4 = (bf16[512,2,128]{2,1,0:T(2,128)(2,1)S(1)}, bf16[512,2,128]{2,1,0:T(2,128)(2,1)}, u32[]{:S(2)}) copy-start(bf16[512,2,128]{2,1,0:T(2,128)(2,1)} %seen.1) | copy-start | bytes 786436
  0.7 53.6 %copy-start.5 = (s32[512,128]{1,0:T(8,128)S(1)}, s32[512,128]{1,0:T(8,128)}, u32[]{:S(2)}) copy-start(s32[512,128]{1,0:T(8,128)} %keep.1) | copy-start | bytes 786436
  0.7 53.6 %copy-start.7 = (s32[15,2,128]{2,1,0:T(2,128)S(1)}, s32[15,2,128]{2,1,0:T(2,128)}, u32[]{:S(2)}) copy-start(s32[15,2,128]{2,1,0:T(2,128)} %pairs.1) | copy-start | bytes 46084
  54.3 1.2 copy-start.2
  55.5 1.6 %copy-start.3 = (bf16[512,8,2,128]{3,2,1,0:T(2,128)(2,1)S(1)}, bf16[512,8,2,128]{3,2,1,0:T(2,128)(2,1)}, u32[]{:S(2)}) copy-start(bf16[512,8,2,128]{3,2,1,0:T(2,128)(2,1)} %param.11) | copy-start | bytes 6291460
  57.1 39.6 %copy-start.8 = (f32[4,2,62,8]{2,3,1,0:T(8,128)S(1)}, f32[4,2,62,8]{2,3,1,0:T(8,128)}, u32[]{:S(2)}) copy-start(f32[4,2,62,8]{2,3,1,0:T(8,128)} %param.18) | copy-start | bytes 47620
  57.1 39.7 %copy-start.9 = (f32[4,2,62,8]{2,3,1,0:T(8,128)S(1)}, f32[4,2,62,8]{2,3,1,0:T(8,128)}, u32[]{:S(2)}) copy-start(f32[4,2,62,8]{2,3,1,0:T(8,128)} %param.20) | copy-start | bytes 47620
  57.1 39.9 %copy-start.10 = (f32[2,2,62,8]{2,3,1,0:T(8,128)S(1)}, f32[2,2,62,8]{2,3,1,0:T(8,128)}, u32[]{:S(2)}) copy-start(f32[2,2,62,8]{2,3,1,0:T(8,128)} %param.19) | copy-start | bytes 23812
  57.1 40.0 %copy-start.13 = (f32[8]{0:T(128)S(1)}, f32[8]{0:T(128)}, u32[]{:S(2)}) copy-start(f32[8]{0:T(128)} %param.21) | copy-start | bytes 100
  94.1 2.3 %copy-start = (f32[129,80,128]{2,1,0:T(8,128)}, f32[129,80,128]{2,1,0:T(8,128)S(1)}, u32[]{:S(2)}) copy-start(f32[129,80,128]{2,1,0:T(8,128)S(1)} %tile_sums.1.sums) | copy-start | bytes 15851524
  97.1 2.5 %copy-start.1 = (f32[129,80,128]{2,1,0:T(8,128)S(1)}, f32[129,80,128]{2,1,0:T(8,128)}, u32[]{:S(2)}) copy-start(f32[129,80,128]{2,1,0:T(8,128)} %copy-done) | copy-start | bytes 15851524

commit v2 on v1

--- a/solution.py
+++ b/solution.py
@@ -1,5 +1,4 @@
 import functools
-import math
 
 import jax
 import jax.numpy as jnp
@@ -28,17 +27,11 @@
     return real, imag
 
 
-def legendre_rows(channels):
-    positions = jnp.arange(channels, dtype=jnp.float32)
-    abscissa = (2.0 * positions - (channels - 1)) / max(channels - 1, 1)
-    return jnp.stack(
-        [
-            jnp.ones_like(abscissa),
-            abscissa,
-            0.5 * (3.0 * abscissa * abscissa - 1.0),
-            0.5 * (5.0 * abscissa * abscissa * abscissa - 3.0 * abscissa),
-        ]
-    )
+def legendre(first, channels):
+    lane = lax.broadcasted_iota(jnp.int32, (1, 2 * HALF), 1)
+    place = (first + lane // HALF).astype(F32)
+    x = (2.0 * place - (channels - 1)) / max(channels - 1, 1)
+    return [jnp.ones_like(x), x, 0.5 * (3.0 * x * x - 1.0), 0.5 * (5.0 * x * x * x - 3.0 * x)]
 
 
 def gram_inverse(channels):
@@ -47,30 +40,42 @@
     return np.linalg.inv(basis @ basis.T)
 
 
-def tile_order(tile_base, bases):
-    tiles = tile_base.shape[0]
-    slots = tiles + GROUP * bases
-    here = jnp.arange(tiles, dtype=jnp.int32)
-    same = (tile_base[:, None] == tile_base[None, :]) & (here[None, :] < here[:, None])
-    rank = jnp.sum(same.astype(jnp.int32), axis=1)
-    rows = jnp.arange(bases, dtype=jnp.int32)
-    counts = jnp.sum((tile_base[None, :] == rows[:, None]).astype(jnp.int32), axis=1)
-    padded = (counts + GROUP - 1) // GROUP * GROUP
-    start = jnp.sum(jnp.where(rows[None, :] < tile_base[:, None], padded[None, :], 0), axis=1)
-    place = start + rank
-    slot = jnp.arange(slots, dtype=jnp.int32)
-    order = jnp.sum(jnp.where(place[None, :] == slot[:, None], here[None, :] - tiles, 0), axis=1) + tiles
-    return order.astype(jnp.int32), (jnp.sum(padded) // GROUP).reshape(1).astype(jnp.int32)
-
-
-def tile_kernel(order, groups, gain_row, home_row, base, sky, seen, keep, pairs, table, out,
-                onehot, sky_s, seen_s, keep_s, gain_s, near_far, terms, sums):
+def tile_order(base, bases, slots):
+    tiles = base.shape[1]
+    padded_bases = -(-bases // 16) * 16
+    member = lax.broadcasted_iota(jnp.int32, (padded_bases, tiles), 0) == base
+    hit = jnp.where(member, 1.0, 0.0)
+    before = jnp.where(lax.broadcasted_iota(jnp.int32, (tiles, tiles), 0)
+                       < lax.broadcasted_iota(jnp.int32, (tiles, tiles), 1), 1.0, 0.0).astype(BF)
+    rank = jnp.dot(hit.astype(BF), before, preferred_element_type=F32)
+    counts = jnp.sum(hit, axis=1, keepdims=True).astype(jnp.int32)
+    groups = lax.shift_right_logical(counts + (GROUP - 1), GROUP.bit_length() - 1).astype(F32)
+    lower = jnp.where(lax.broadcasted_iota(jnp.int32, (padded_bases, padded_bases), 1)
+                      < lax.broadcasted_iota(jnp.int32, (padded_bases, padded_bases), 0), 1.0, 0.0).astype(BF)
+    start = jnp.dot(lower, jnp.broadcast_to(groups, (padded_bases, tiles)).astype(BF),
+                    preferred_element_type=F32)
+    where = jnp.sum(jnp.where(member, rank + GROUP * start, 0.0), axis=0, keepdims=True).astype(jnp.int32)
+    chosen = jnp.where(lax.broadcasted_iota(jnp.int32, (slots, tiles), 0) == where, 1.0, 0.0).astype(BF)
+    tile = lax.broadcasted_iota(jnp.int32, (8, tiles), 1)
+    kind = lax.broadcasted_iota(jnp.int32, (8, tiles), 0)
+    digits = jnp.where(kind == 0, lax.shift_right_logical(tile, 4),
+                       jnp.where(kind == 1, jnp.bitwise_and(tile, 15), 1)).astype(F32).astype(BF)
+    found = lax.dot_general(digits, chosen, (((1,), (1,)), ((), ())), preferred_element_type=F32)
+    named = jnp.where(found[2:3] > 0.5, 16.0 * found[0:1] + found[1:2], float(tiles)).astype(jnp.int32)
+    total = jnp.broadcast_to(jnp.sum(groups, axis=0, keepdims=True), (1, 128)).astype(jnp.int32)
+    return named, total
+
+
+def tile_kernel(half_count, order, groups, owner, channel, base, sky, seen, keep, pairs, table, out, onehot, *buffers):
     tiles, coupled, rows = sky.shape
     directions = coupled // 2
     bases = pairs.shape[0]
     real, imag = term_rows(directions)
     n_terms = directions * directions + 2 * directions
     devices = out.shape[0] - 1
+    channels_here = table.shape[0] // (devices // 2)
+    chans = devices // 2
+    buffers = (buffers[0::2], buffers[1::2])
 
     station = lax.rem(lax.broadcasted_iota(jnp.int32, (2 * HALF, rows), 0), HALF)
     for b in range(bases):
@@ -84,17 +89,23 @@
     lax.fori_loop(0, devices + 1, clear, 0)
     lane = lax.broadcasted_iota(jnp.int32, (1, 2 * HALF), 1)
 
-    def one_group(g, carry):
+    def chosen(g):
+        first = order[0, jnp.maximum(g, 0) * GROUP]
+        return onehot.at[base[jnp.minimum(first, tiles - 1)]]
+
+    def load(g, into):
+        sky_s, seen_s, keep_s, gain_s, near_far, _, _ = buffers[into]
         for t in range(GROUP):
-            named = order[g * GROUP + t]
+            named = order[0, g * GROUP + t]
             tile = jnp.where(named < tiles, named, 0)
             sky_s[pl.ds(t, coupled, stride=GROUP), :] = sky[tile].astype(F32)
             seen_s[pl.ds(t, 2, stride=GROUP), :] = seen[tile].astype(F32)
             keep_s[pl.ds(t, 1), :] = keep[pl.ds(tile, 1), :]
-            gain_s[pl.ds(t, coupled, stride=GROUP), :] = table[gain_row[tile]].astype(F32)
-        chosen = onehot.at[base[order[g * GROUP]]]
-        near_far[...] = jnp.dot(gain_s[...].astype(BF), chosen[...], preferred_element_type=F32)
-
+            gain_s[pl.ds(t, coupled, stride=GROUP), :] = table[owner[tile] * channels_here + channel[tile]].astype(F32)
+        near_far[...] = jnp.dot(gain_s[...].astype(BF), chosen(g)[...], preferred_element_type=F32)
+
+    def products(of):
+        sky_s, seen_s, keep_s, _, near_far, terms, _ = buffers[of]
         kept = keep_s[...] > 0
 
         def block(ref, i):
@@ -107,8 +118,8 @@
         for k in range(directions):
             c_r = jnp.where(kept, block(sky_s, 2 * k), 0.0)
             c_i = jnp.where(kept, block(sky_s, 2 * k + 1), 0.0)
-            p_r, p_i = (near_far[(2 * k + c) * GROUP:(2 * k + c + 1) * GROUP, :rows] for c in range(2))
-            q_r, q_i = (near_far[(2 * k + c) * GROUP:(2 * k + c + 1) * GROUP, rows:] for c in range(2))
+            p_r, p_i = (block(near_far, c * directions + k)[:, :rows] for c in range(2))
+            q_r, q_i = (block(near_far, c * directions + k)[:, rows:] for c in range(2))
             x_r = c_r * q_r + c_i * q_i
             x_i = c_i * q_r - c_r * q_i
             a_r.append(x_r)
@@ -124,7 +135,6 @@
 
         for side, (v_r, v_i, w_r, w_i) in enumerate(
                 ((a_r, a_i, res_r, res_i), (b_r, b_i, res_r, -res_i))):
-            made = [None] * n_terms
             pending = {}
 
             def put(j, value):
@@ -144,22 +154,37 @@
             for k in range(directions):
                 put(first + directions + k, v_r[k] * w_i - v_i[k] * w_r)
 
-        sums[...] = lax.dot_general(terms[...], chosen[...], (((1,), (1,)), ((), ())),
+    def station_sums(g, of):
+        terms, sums = buffers[of][5:]
+        sums[...] = lax.dot_general(terms[...], chosen(g)[...], (((1,), (1,)), ((), ())),
                                     preferred_element_type=F32)
+
+    def add_up(g, of):
+        sums = buffers[of][6]
         for t in range(GROUP):
-            named = order[g * GROUP + t]
+            named = jnp.where(g < 0, tiles, order[0, jnp.maximum(g, 0) * GROUP + t])
             tile = jnp.where(named < tiles, named, 0)
-            home = home_row[tile]
-            row = jnp.where(named < tiles, lax.shift_right_logical(home, 1), devices)
-            part = jnp.where(lane // HALF == jnp.bitwise_and(home, 1),
+            mine = channel[tile]
+            row = jnp.where(named < tiles, (mine // half_count) * chans + owner[tile], devices)
+            part = jnp.where(lane // HALF == lax.rem(mine, half_count),
                              sums[pl.ds(t, n_terms, stride=GROUP), :], 0.0)
             out[row] = out[row] + part
-        return carry
-
-    lax.fori_loop(0, groups[0], one_group, 0)
-
-
-def tile_sums(sky, seen, keep, order, groups, gain_row, home_row, base, pairs, table, devices):
+
+    def step(g, of):
+        station_sums(g - 2, of)
+        add_up(g - 3, 1 - of)
+        load(g, of)
+        products(1 - of)
+
+    def two(i, carry):
+        step(2 * i, 0)
+        step(2 * i + 1, 1)
+        return carry
+
+    lax.fori_loop(0, (groups[0, 0] + 4) // 2, two, 0)
+
+
+def tile_sums(sky, seen, keep, order, groups, owner, channel, base, pairs, table, devices, half_count):
     tiles, directions, _, rows = sky.shape
     n_terms = directions * directions + 2 * directions
     bases = pairs.shape[0]
@@ -167,23 +192,24 @@
     vmem = pl.BlockSpec(memory_space=pltpu.VMEM)
     coupled = 2 * directions
     return pl.pallas_call(
-        tile_kernel,
+        functools.partial(tile_kernel, half_count),
         out_shape=jax.ShapeDtypeStruct((devices + 1, n_terms, 2 * HALF), F32),
         in_specs=[smem] * 5 + [vmem] * 5,
         out_specs=vmem,
-        scratch_shapes=[
-            pltpu.VMEM((bases, 2 * HALF, 2 * rows), BF),
-            pltpu.VMEM((coupled * GROUP, rows), F32),
-            pltpu.VMEM((2 * GROUP, rows), F32),
-            pltpu.VMEM((GROUP, rows), jnp.int32),
-            pltpu.VMEM((coupled * GROUP, 2 * HALF), F32),
-            pltpu.VMEM((coupled * GROUP, 2 * rows), F32),
-            pltpu.VMEM((n_terms * GROUP, 2 * rows), BF),
-            pltpu.VMEM((n_terms * GROUP, 2 * HALF), F32),
+        scratch_shapes=[pltpu.VMEM((bases, 2 * HALF, 2 * rows), BF)] + [
+            shape for shape in (
+                pltpu.VMEM((coupled * GROUP, rows), F32),
+                pltpu.VMEM((2 * GROUP, rows), F32),
+                pltpu.VMEM((GROUP, rows), jnp.int32),
+                pltpu.VMEM((coupled * GROUP, 2 * HALF), F32),
+                pltpu.VMEM((coupled * GROUP, 2 * rows), F32),
+                pltpu.VMEM((n_terms * GROUP, 2 * rows), BF),
+                pltpu.VMEM((n_terms * GROUP, 2 * HALF), F32),
+            ) for _ in range(2)
         ],
-        compiler_params=pltpu.CompilerParams(vmem_limit_bytes=40 * 1024 * 1024),
+        compiler_params=pltpu.CompilerParams(vmem_limit_bytes=18 * 1024 * 1024),
         name="tile_sums",
-    )(order, groups, gain_row, home_row, base, sky.reshape(tiles, coupled, rows), seen, keep, pairs, table)
+    )(order, groups, owner, channel, base, sky.reshape(tiles, coupled, rows), seen, keep, pairs, table)
 
 
 def eliminate(total, target, rho, full, directions):
@@ -256,10 +282,17 @@
     return jnp.where(lax.rem(i, 2) == 0, i // 2 + 1, nz - 1 - i // 2)
 
 
-def gather_kernel(nx, nz, mine, table, z_recv, z_send, x_recv, x_send, c_recv, c_send):
+def gather_kernel(nx, nz, bases, gains, base, table, order, groups, wide, mine,
+                  z_recv, z_send, x_recv, x_send, c_recv, c_send):
     x, z, s = place()
     here, half = mine.shape[0], mine.shape[0] // 2
+    stations = gains.shape[2]
     barrier, count = meet(x, z, s, nx, nz, False)
+    wide[...] = jnp.zeros(wide.shape, F32)
+    head = gains[...].astype(BF).astype(F32)
+    wide[:, :, :stations] = head
+    wide[:, :, HALF:HALF + stations] = gains[...] - head
+    mine[...] = wide[...].astype(BF)
     table[pl.ds((x * nz + z) * here + s * half, half)] = mine[pl.ds(s * half, half)]
     pl.semaphore_wait(barrier, count)
 
@@ -283,6 +316,7 @@
         return sender(src, block(x, zz), x_send.at[e, d], x_recv.at[e, d], lax.rem(x + e, nx), z, s)
     for e in range(1, nx):
         x_copy(own, z, 0, e).start()
+    order[...], groups[...] = tile_order(base[...], bases, order.shape[1])
 
     def pass_on(i, carry):
         d = outward(i, nz)
@@ -322,18 +356,23 @@
         c_copy(e, s).wait_send()
 
 
-def gather_gains(mine, nx, nz):
+def gather_gains(gains, base, bases, nx, nz):
     vmem = pl.BlockSpec(memory_space=pltpu.VMEM)
     dma = pltpu.SemaphoreType.DMA
+    here, rows, _ = gains.shape
+    slots = -(-(base.shape[1] + GROUP * (bases + 6)) // 128) * 128
     return pl.pallas_call(
-        functools.partial(gather_kernel, nx, nz),
-        out_shape=jax.ShapeDtypeStruct((nx * nz * mine.shape[0],) + mine.shape[1:], mine.dtype),
-        in_specs=[vmem],
-        out_specs=vmem,
-        scratch_shapes=[dma((nz,)), dma((nz,)), dma((nx, nz)), dma((nx, nz)), dma((nx,)), dma((nx,))],
-        compiler_params=pltpu.CompilerParams(collective_id=0, has_side_effects=True),
+        functools.partial(gather_kernel, nx, nz, bases),
+        out_shape=(jax.ShapeDtypeStruct((nx * nz * here, rows, 2 * HALF), BF),
+                   jax.ShapeDtypeStruct((1, slots), jnp.int32), jax.ShapeDtypeStruct((1, 128), jnp.int32)),
+        in_specs=[vmem, vmem],
+        out_specs=(vmem, vmem, vmem),
+        scratch_shapes=[pltpu.VMEM((here, rows, 2 * HALF), F32), pltpu.VMEM((here, rows, 2 * HALF), BF),
+                        dma((nz,)), dma((nz,)), dma((nx, nz)), dma((nx, nz)), dma((nx,)), dma((nx,))],
+        compiler_params=pltpu.CompilerParams(collective_id=0, has_side_effects=True,
+                                             vmem_limit_bytes=8 * 1024 * 1024),
         name="gather_gains",
-    )(mine)
+    )(gains, base)
 
 
 def packed(v, plain):
@@ -348,16 +387,27 @@
     return jnp.concatenate([v[:plain], v[plain:mid] + v[mid:]], axis=0)
 
 
-def finish_kernel(nx, nz, inverse, sums, gain, dual, cons, basis, rho, gain_new, cons_new, dual_new,
-                  peer, x_out, x_in, z_out, z_in, own_z, total, full, part_out, part_in, ring_in, last_in,
-                  c_send, c_recv, x_send, x_recv, z_send, z_recv, p_send, p_recv, r_send, r_recv, l_send, l_recv):
+def finish_kernel(nx, nz, inverse, sums, gains, duals, cons, rho, gain_new, cons_new, dual_new,
+                  peer, two_out, two_in, x_out, x_in, z_out, z_in, own_z, total, full, wide,
+                  part_out, part_in, ring_in, last_in,
+                  c_send, c_recv, t_send, t_recv, x_send, x_recv, z_send, z_recv,
+                  p_send, p_recv, r_send, r_recv, l_send, l_recv):
     x, z, s = place()
     directions = rho.shape[0]
-    degrees = basis.shape[0]
+    degrees, _, stations = cons.shape
+    half_count = duals.shape[0]
     plain = directions * directions
     chunk = 4
     nodes = nx * nz
     barrier, count = meet(x, z, s, nx, nz, True)
+
+    wide[...] = jnp.zeros(wide.shape, F32)
+    for h in range(half_count):
+        wide[0, :, h * HALF:h * HALF + stations] = gains[s * half_count + h]
+        wide[1, :, h * HALF:h * HALF + stations] = duals[h]
+        for d in range(degrees):
+            wide[2 + d, :, h * HALF:h * HALF + stations] = cons[d]
+    basis = legendre(((x * nz + z) * 2 + s) * half_count, 2 * nodes * half_count)
     pl.semaphore_wait(barrier, count)
 
     def far(i):
@@ -368,45 +418,73 @@
         xx = lax.rem(x + e, nx)
         return sender(sums.at[pl.ds(h * nodes + xx * nz, nz)], peer.at[pl.ds(xx * nz, nz)],
                       c_send.at[e], c_recv.at[e], x, z, 1 - s)
-    order = (2, 1, 3, 0)
+    across, right, left_ = nx // 2, 1, nx - 1
+    order = (across, right, left_, 0)
     for e in order:
         c_copy(e, 1 - s).start()
 
     def pair_sum(xx, zz):
         return sums[s * nodes + xx * nz + zz] + peer[xx * nz + zz]
 
-    def x_copy(e, c):
+    chunks = nz // chunk
+    share = chunk // 2
+    def t_copy(side, c):
+        at = pl.ds(c * chunk + side * share, share)
+        return sender(two_out.at[at], two_in.at[at], t_send.at[side, c], t_recv.at[side, c],
+                      lax.rem(x + (right, left_)[side], nx), z, s)
+    c_copy(across, s).wait_recv()
+
+    def fill_two(c, carry):
+        def one(j, inner):
+            i = c * chunk + j
+            two_out[i] = packed(pair_sum(lax.rem(x + across, nx), lax.rem(z + far(i), nz)), plain)
+            return inner
+        lax.fori_loop(0, chunk, one, 0)
+        for side in range(2):
+            t_copy(side, c).start()
+        return carry
+    lax.fori_loop(0, chunks, fill_two, 0)
+
+    def x_copy(side, c):
         at = pl.ds(c * chunk, chunk)
-        return sender(x_out.at[e, at], x_in.at[e, at], x_send.at[e, c], x_recv.at[e, c],
-                      lax.rem(x + e, nx), z, s)
-    chunks = nz // chunk
-    for e in order[:-1]:
-        c_copy(e, s).wait_recv()
+        return sender(x_out.at[side, at], x_in.at[side, at], x_send.at[side, c], x_recv.at[side, c],
+                      lax.rem(x + (right, left_)[side], nx), z, s)
+    c_copy(right, s).wait_recv()
+    c_copy(left_, s).wait_recv()
+
+    def fill_x(c, carry):
+        for side in range(2):
+            t_copy(side, c).wait_recv()
+            xx = lax.rem(x + (right, left_)[side], nx)
+
+            def relayed(j, inner):
+                i = c * chunk + side * share + j
+                x_out[side, i] = packed(pair_sum(xx, lax.rem(z + far(i), nz)) + unpacked(two_in[i], plain), plain)
+                return inner
+
+            def plainly(j, inner):
+                i = c * chunk + (1 - side) * share + j
+                x_out[side, i] = packed(pair_sum(xx, lax.rem(z + far(i), nz)), plain)
+                return inner
+            lax.fori_loop(0, share, relayed, 0)
+            lax.fori_loop(0, share, plainly, 0)
+            x_copy(side, c).start()
+        return carry
+    lax.fori_loop(0, chunks, fill_x, 0)
     c_copy(0, s).wait_recv()
-
-    def fill_x(c, carry):
-        for e in order[:-1]:
-            def one(j, inner):
-                i = c * chunk + j
-                x_out[e, i] = packed(pair_sum(lax.rem(x + e, nx), lax.rem(z + far(i), nz)), plain)
-                return inner
-            lax.fori_loop(0, chunk, one, 0)
-            x_copy(e, c).start()
-        return carry
-    lax.fori_loop(0, chunks, fill_x, 0)
 
     def z_copy(i):
         return sender(z_out.at[i], z_in.at[i], z_send.at[i], z_recv.at[i], x, lax.rem(z + far(i), nz), s)
 
     def fill_z(c, carry):
-        for e in order[:-1]:
-            x_copy(e, c).wait_recv()
+        for side in range(2):
+            x_copy(side, c).wait_recv()
 
         def one(j, inner):
             i = c * chunk + j
             acc = pair_sum(x, lax.rem(z + far(i), nz))
-            for e in range(1, nx):
-                acc = acc + unpacked(x_in[e, i], plain)
+            for side in range(2):
+                acc = acc + unpacked(x_in[side, i], plain)
             z_out[i] = packed(acc, plain)
             own_z[...] = acc
 
@@ -426,15 +504,17 @@
     lax.fori_loop(0, nz - 1, take_z, 0)
 
     rho2 = jnp.concatenate([rho[...], rho[...]], axis=0)
-    anchor = sum(basis[d:d + 1, :] * cons[d] for d in range(degrees))
-    target = total[plain:, :] - dual[...] - rho2 * (gain[...] - anchor)
-    new = gain[...] + eliminate(total, target, rho[...], full, directions)
-    gain_new[...] = new
-    weighted = new + dual[...] / rho2
+    gain, dual = wide[0], wide[1]
+    anchor = sum(basis[d] * wide[2 + d] for d in range(degrees))
+    target = total[plain:, :] - dual - rho2 * (gain - anchor)
+    new = gain + eliminate(total, target, rho[...], full, directions)
+    for h in range(half_count):
+        gain_new[h] = new[:, h * HALF:h * HALF + stations]
+    weighted = new + dual / rho2
     left = lax.broadcasted_iota(jnp.int32, (2 * directions, 2 * HALF), 1) < HALF
 
     def folded(d):
-        part = basis[d:d + 1, :] * weighted
+        part = basis[d] * weighted
         return part + pltpu.roll(part, HALF, axis=1)
     pair = degrees // 2
     both = jnp.concatenate([jnp.where(left, folded(d), folded(d + pair)) for d in range(pair)], axis=0)
@@ -499,17 +579,20 @@
     fit = None
     for d in range(degrees):
         coeff = sum(inverse[d][q] * summed[q] for q in range(degrees))
-        cons_new[d] = coeff
-        term = basis[d:d + 1, :] * coeff
+        cons_new[d] = coeff[:, :stations]
+        term = basis[d] * coeff
         fit = term if fit is None else fit + term
-    dual_new[...] = dual[...] + rho2 * (new - fit)
+    dual_out = dual + rho2 * (new - fit)
+    for h in range(half_count):
+        dual_new[h] = dual_out[:, h * HALF:h * HALF + stations]
 
     for e in range(nx):
         c_copy(e, 1 - s).wait_send()
 
     def sent_x(c, carry):
-        for e in range(1, nx):
-            x_copy(e, c).wait_send()
+        for side in range(2):
+            t_copy(side, c).wait_send()
+            x_copy(side, c).wait_send()
         return carry
     lax.fori_loop(0, chunks, sent_x, 0)
 
@@ -523,91 +606,70 @@
         l_copy(e, f, me).wait_send()
 
 
-def finish(sums, gain, dual, cons, basis, rho, inverse, nx, nz):
+def finish(sums, gains, duals, cons, rho, inverse, nx, nz):
     vmem = pl.BlockSpec(memory_space=pltpu.VMEM)
     dma = pltpu.SemaphoreType.DMA
-    degrees, directions = basis.shape[0], rho.shape[0]
+    degrees, rows, _ = cons.shape
     terms, lanes = sums.shape[1:]
-    wire = terms + 2 * directions
+    wire = terms + rows
     pieces = 2 * nx
-    piece = degrees * 2 * directions // 2 // pieces
+    piece = degrees * rows // 2 // pieces
     chunks = nz // 4
     return pl.pallas_call(
         functools.partial(finish_kernel, nx, nz, inverse),
-        out_shape=(jax.ShapeDtypeStruct(gain.shape, F32), jax.ShapeDtypeStruct(cons.shape, F32),
-                   jax.ShapeDtypeStruct(gain.shape, F32)),
-        in_specs=[vmem] * 6,
+        out_shape=(jax.ShapeDtypeStruct(duals.shape, F32), jax.ShapeDtypeStruct(cons.shape, F32),
+                   jax.ShapeDtypeStruct(duals.shape, F32)),
+        in_specs=[vmem] * 5,
         out_specs=(vmem, vmem, vmem),
         scratch_shapes=[
             pltpu.VMEM((nx * nz, terms, lanes), F32),
-            pltpu.VMEM((nx, nz, wire, lanes), BF),
-            pltpu.VMEM((nx, nz, wire, lanes), BF),
+            pltpu.VMEM((nz, wire, lanes), BF),
+            pltpu.VMEM((nz, wire, lanes), BF),
+            pltpu.VMEM((2, nz, wire, lanes), BF),
+            pltpu.VMEM((2, nz, wire, lanes), BF),
             pltpu.VMEM((nz, wire, lanes), BF),
             pltpu.VMEM((nz, wire, lanes), BF),
             pltpu.VMEM((terms, lanes), F32),
             pltpu.VMEM((terms, lanes), F32),
-            pltpu.VMEM((2, directions * directions, lanes), F32),
+            pltpu.VMEM((2, rows * rows // 4, lanes), F32),
+            pltpu.VMEM((2 + degrees, rows, lanes), F32),
             pltpu.VMEM((pieces, piece, lanes), F32),
             pltpu.VMEM((pieces, piece, lanes), F32),
             pltpu.VMEM((nz, piece, lanes), F32),
             pltpu.VMEM((pieces, piece, lanes), F32),
-            dma((nx,)), dma((nx,)), dma((nx, chunks)), dma((nx, chunks)), dma((nz,)), dma((nz,)),
+            dma((nx,)), dma((nx,)), dma((2, chunks)), dma((2, chunks)), dma((2, chunks)), dma((2, chunks)),
+            dma((nz,)), dma((nz,)),
             dma((pieces,)), dma((pieces,)), dma((nz,)), dma((nz,)), dma((pieces,)), dma((pieces,)),
         ],
         compiler_params=pltpu.CompilerParams(collective_id=1, has_side_effects=True,
-                                             vmem_limit_bytes=40 * 1024 * 1024),
+                                             vmem_limit_bytes=18 * 1024 * 1024),
         name="finish",
-    )(sums, gain, dual, cons, basis, rho)
-
-
-def to_lanes(x):
-    h, c, s, k = x.shape
-    x = jnp.pad(x, ((0, 0), (0, 0), (0, HALF - s), (0, 0)))
-    return jnp.transpose(x, (1, 3, 0, 2)).reshape(c * k, h * HALF)
-
-
-def from_lanes(x, stations):
-    rows, lanes = x.shape
-    x = x.reshape(2, rows // 2, lanes // HALF, HALF)[..., :stations]
-    return jnp.transpose(x, (2, 0, 3, 1))
-
-
-def gain_table(gains):
-    n, c, s, k = gains.shape
-    x = jnp.pad(jnp.transpose(gains, (0, 3, 1, 2)).reshape(n, k * c, s), ((0, 0), (0, 0), (0, HALF - s)))
-    head = lax.reduce_precision(x, 8, 7)
-    return jnp.concatenate([head, x - head], axis=-1).astype(BF)
+    )(sums, gains, duals, cons, rho)
+
+
+def to_rows(x):
+    n, c, s, k = x.shape
+    return jnp.transpose(x, (0, 1, 3, 2)).reshape(n, c * k, s)
+
+
+def from_rows(x):
+    n, rows, s = x.shape
+    return jnp.transpose(x.reshape(n, 2, rows // 2, s), (0, 1, 3, 2))
 
 
 def body(sky, seen, keep, tile_owner, tile_channel, tile_base, pairs, gains, duals, consensus, rho):
-    channels_here, _, stations, directions = gains.shape
-    chan_count = lax.axis_size(("chan_0", "chan_1"))
+    channels_here, _, _, directions = gains.shape
+    nx, nz = lax.axis_size(XS), lax.axis_size(ZS)
     sub_count = lax.axis_size("sub")
     half_count = channels_here // sub_count
-    devices = chan_count * sub_count
-    sub_index = lax.axis_index("sub")
-    chan_index = lax.axis_index(("chan_0", "chan_1"))
-
-    nx, nz = lax.axis_size(XS), lax.axis_size(ZS)
-    table = gather_gains(gain_table(gains), nx, nz)
-    owner = tile_owner[:, 0]
-    order, groups = tile_order(tile_base, pairs.shape[0])
-    home = ((tile_channel // half_count) * chan_count + owner) * half_count + tile_channel % half_count
-    sums = tile_sums(sky, seen, keep, order, groups, owner * channels_here + tile_channel, home,
-                     tile_base, pairs, table, devices)
-
-    my_gains = lax.dynamic_slice_in_dim(gains, sub_index * half_count, half_count, 0)
-    channels = channels_here * chan_count
-    first_channel = (chan_index * sub_count + sub_index) * half_count
-    my_basis = lax.dynamic_slice_in_dim(legendre_rows(channels), first_channel, half_count, 1)
-    basis = jnp.repeat(my_basis, HALF, axis=1)
-    cons = jax.vmap(lambda c: to_lanes(jnp.stack([c, c])))(consensus)
-    gain_l, dual_l = to_lanes(my_gains), to_lanes(duals)
-    rho_l = jnp.broadcast_to(rho[:, None], (directions, 2 * HALF))
-    new_l, fitted, dual_new = finish(sums, gain_l, dual_l, cons, basis, rho_l,
-                                     gram_inverse(channels).tolist(), nx, nz)
-    consensus_new = jax.vmap(lambda x: from_lanes(x, stations)[0])(fitted)
-    return from_lanes(new_l, stations), consensus_new, from_lanes(dual_new, stations)
+    gain_rows = to_rows(gains)
+    table, order, groups = gather_gains(gain_rows, tile_base.reshape(1, -1), pairs.shape[0], nx, nz)
+    sums = tile_sums(sky, seen, keep, order, groups, tile_owner[:, 0], tile_channel, tile_base, pairs, table,
+                     nx * nz * sub_count, half_count)
+    rho_rows = jnp.broadcast_to(rho[:, None], (directions, 2 * HALF))
+    gain_new, cons_new, dual_new = finish(sums, gain_rows, to_rows(duals), to_rows(consensus), rho_rows,
+                                          gram_inverse(channels_here * nx * nz).tolist(), nx, nz)
+    return from_rows(gain_new), from_rows(cons_new), from_rows(dual_new)
 
 
 def solution(mesh):

time: 155 us -> 132 us (0.85)
  Pallas kernels: 137 us -> 121 us
  other arithmetic: 3.58 us -> 0 us
  between operations: 3.47 us -> 0.7 us
    pallas_call x2, Pallas kernels: 83.6 us -> 69.5 us  [the longest x1 44.9 us: gather_gains(): pl.pallas_call(functools.partial(gather_kernel, nx, nz, bases), out_shape...]
    reduce_sum x5 -> x0, other arithmetic: 2.73 us -> none  [the longest x1 0.86 us: tile_order(): jnp.sum((tile_base[None, :] == rows[:, None]).astype(jnp.int32), axis=1)]
    unnamed x31 -> x29, local copies, waits for them, and re-layouts: 8.89 us -> 9.52 us
where the time goes in v2:
time: 132 us
  Pallas kernels  121 us (92%)
  local copies, waits for them, and re-layouts  9.59 us (7%)
    pallas_call x1, Pallas kernels, finish(): pl.pallas_call(functools.partial(finish_kernel, nx, nz, inverse), out_sha...  51.7 us
    pallas_call x1, Pallas kernels, gather_gains(): pl.pallas_call(functools.partial(gather_kernel, nx, nz, bases), out_shape...  44.9 us
    pallas_call x1, Pallas kernels, tile_sums(): pl.pallas_call(functools.partial(tile_kernel, half_count), out_shape=jax....  24.6 us
    unnamed x29, local copies, waits for them, and re-layouts  9.52 us

profile of v2, /device:TPU:33, one launch (start us, length us, event | category | flops | bytes accessed | tf_op | source)
XLA Modules:
  0.0 131.6 jit_solution(16217029429114000665)
XLA Ops:
  0.6 0.0 copy-start.12
  0.6 0.0 copy-start.3
  0.7 0.8 copy-done.3
  1.4 0.0 copy-start.8
  1.4 0.7 copy-done.8
  2.1 44.9 %gather_gains.1 = (bf16[256,16,128]{2,1,0:T(8,128)(2,1)S(1)}, s32[1,768]{1,0:T(1,128)S(1)}, s32[1,128]{1,0:T(1,128)S(1)}) custom-call(f32[4,16,62]{2,1,0:T(8,128)S(1)} %bitcast.22, s32[1,512]{1,0:T(1,128)S(1)} %bitcast.29), custom_call_target="tpu_custom_call" | custom-call | tf_op jit(solution)/shard_map/gather_gains/pallas_call | solution.py:364
  47.0 0.0 copy-start
  47.0 1.6 %copy-done = bf16[512,8,2,128]{3,2,1,0:T(2,128)(2,1)S(1)} copy-done((bf16[512,8,2,128]{3,2,1,0:T(2,128)(2,1)S(1)}, bf16[512,8,2,128]{3,2,1,0:T(2,128)(2,1)}, u32[]{:S(2)}) %copy-start) | copy-done | bytes 2097176
  48.6 0.9 copy-done.1
  49.6 0.9 copy-done.2
  50.5 0.7 copy-done.7
  51.2 0.7 copy-done.9
  51.9 0.7 copy-done.10
  52.6 0.7 copy-done.11
  53.3 24.6 %tile_sums.1.sums = f32[129,80,128]{2,1,0:T(8,128)S(1)} custom-call(s32[1,768]{1,0:T(1,128)S(1)} %get-tuple-element.9.order, s32[1,128]{1,0:T(1,128)S(1)} %get-tuple-element.10.groups, s32[512]{0:T(512)S(1)} %bitcast.30, s32[512]{0:T(512)S(1)} %copy-done.11, s32[512]{0:T(512)S(1)} %copy-done.9, bf16[512,16,128]{2,1,0:T(8,128)(2,1)S(1)} %bitcast.21, ...), custom_call_target="tpu_custom_call" | custom-call | tf_op jit(solution)/shard_map/tile_sums/pallas_call | solution.py:194
  77.9 0.0 copy-done.12
  77.9 0.1 broadcast_in_dim.2.rho
  78.0 0.0 copy-done.4
  78.0 0.0 copy-done.5
  78.0 0.0 copy-done.6
  78.0 51.7 %finish.1 = (f32[2,16,62]{2,1,0:T(8,128)S(1)}, f32[4,16,62]{2,1,0:T(8,128)S(1)}, f32[2,16,62]{2,1,0:T(8,128)S(1)}) custom-call(f32[129,80,128]{2,1,0:T(8,128)S(1)} %tile_sums.1.sums, f32[4,16,62]{2,1,0:T(8,128)S(1)} %bitcast.23, f32[2,16,62]{2,1,0:T(8,128)S(1)} %bitcast.26, f32[4,16,62]{2,1,0:T(8,128)S(1)} %bitcast.24, f32[8,128]{1,0:T(8,128)S(1)} %broadcast_in_dim.2.rho), custom_call_target="tpu_custom_call" | custom-call | tf_op jit(solution)/shard_map/finish/pallas_call | solution.py:618
  129.7 0.6 copy.17
  130.4 0.6 copy.18
  131.0 0.6 copy.19
  (9 shorter events, 0.0 us)
Async XLA Ops:
  0.6 77.3 %copy-start.12 = (f32[8]{0:T(128)S(1)}, f32[8]{0:T(128)}, u32[]{:S(2)}) copy-start(f32[8]{0:T(128)} %param.21) | copy-start | bytes 100
  0.6 0.8 copy-start.3
  1.4 0.7 copy-start.8
  2.1 75.9 %copy-start.4 = (f32[4,2,62,8]{2,3,1,0:T(8,128)S(1)}, f32[4,2,62,8]{2,3,1,0:T(8,128)}, u32[]{:S(2)}) copy-start(f32[4,2,62,8]{2,3,1,0:T(8,128)} %param.18) | copy-start | bytes 47620
  47.0 1.6 %copy-start = (bf16[512,8,2,128]{3,2,1,0:T(2,128)(2,1)S(1)}, bf16[512,8,2,128]{3,2,1,0:T(2,128)(2,1)}, u32[]{:S(2)}) copy-start(bf16[512,8,2,128]{3,2,1,0:T(2,128)(2,1)} %param.11) | copy-start | bytes 6291460
  48.6 0.9 copy-start.1
  49.6 0.9 copy-start.2
  50.5 0.7 copy-start.7
  51.2 0.7 copy-start.9
  51.9 0.7 copy-start.10
  52.6 0.7 copy-start.11
  53.3 24.7 %copy-start.5 = (f32[4,2,62,8]{2,3,1,0:T(8,128)S(1)}, f32[4,2,62,8]{2,3,1,0:T(8,128)}, u32[]{:S(2)}) copy-start(f32[4,2,62,8]{2,3,1,0:T(8,128)} %param.20) | copy-start | bytes 47620
  53.3 24.7 %copy-start.6 = (f32[2,2,62,8]{2,3,1,0:T(8,128)S(1)}, f32[2,2,62,8]{2,3,1,0:T(8,128)}, u32[]{:S(2)}) copy-start(f32[2,2,62,8]{2,3,1,0:T(8,128)} %param.19) | copy-start | bytes 23812

commit v3 on v2

--- a/solution.py
+++ b/solution.py
@@ -66,7 +66,13 @@
     return named, total
 
 
-def tile_kernel(half_count, order, groups, owner, channel, base, sky, seen, keep, pairs, table, out, onehot, *buffers):
+def tile_kernel(half_count, order, groups, table, far_owner, far_channel, far_base, far_sky, far_seen, far_keep,
+                far_pairs, out, onehot, owner, channel, base, sky, seen, keep, pairs, arrived, *buffers):
+    fetched = [pltpu.make_async_copy(src, dst, arrived.at[i]) for i, (src, dst) in enumerate((
+        (far_pairs, pairs), (far_base, base), (far_owner, owner), (far_channel, channel),
+        (far_sky, sky), (far_seen, seen), (far_keep, keep)))]
+    for copy in fetched:
+        copy.start()
     tiles, coupled, rows = sky.shape
     directions = coupled // 2
     bases = pairs.shape[0]
@@ -77,16 +83,19 @@
     chans = devices // 2
     buffers = (buffers[0::2], buffers[1::2])
 
+    def clear(i, carry):
+        out[i] = jnp.zeros((n_terms, 2 * HALF), F32)
+        return carry
+    lax.fori_loop(0, devices + 1, clear, 0)
+    fetched[0].wait()
     station = lax.rem(lax.broadcasted_iota(jnp.int32, (2 * HALF, rows), 0), HALF)
     for b in range(bases):
         for side in range(2):
             onehot[b, :, side * rows:(side + 1) * rows] = jnp.where(
                 station == pairs[b, side:side + 1, :], 1.0, 0.0).astype(BF)
 
-    def clear(i, carry):
-        out[i] = jnp.zeros((n_terms, 2 * HALF), F32)
-        return carry
-    lax.fori_loop(0, devices + 1, clear, 0)
+    for copy in fetched[1:]:
+        copy.wait()
     lane = lax.broadcasted_iota(jnp.int32, (1, 2 * HALF), 1)
 
     def chosen(g):
@@ -190,13 +199,20 @@
     bases = pairs.shape[0]
     smem = pl.BlockSpec(memory_space=pltpu.SMEM)
     vmem = pl.BlockSpec(memory_space=pltpu.VMEM)
+    hbm = pl.BlockSpec(memory_space=pltpu.HBM)
     coupled = 2 * directions
     return pl.pallas_call(
         functools.partial(tile_kernel, half_count),
         out_shape=jax.ShapeDtypeStruct((devices + 1, n_terms, 2 * HALF), F32),
-        in_specs=[smem] * 5 + [vmem] * 5,
+        in_specs=[smem] * 2 + [vmem] + [hbm] * 7,
         out_specs=vmem,
-        scratch_shapes=[pltpu.VMEM((bases, 2 * HALF, 2 * rows), BF)] + [
+        scratch_shapes=[
+            pltpu.VMEM((bases, 2 * HALF, 2 * rows), BF),
+            pltpu.SMEM((tiles,), jnp.int32), pltpu.SMEM((tiles,), jnp.int32), pltpu.SMEM((tiles,), jnp.int32),
+            pltpu.VMEM((tiles, coupled, rows), BF), pltpu.VMEM(seen.shape, BF),
+            pltpu.VMEM(keep.shape, jnp.int32), pltpu.VMEM(pairs.shape, jnp.int32),
+            pltpu.SemaphoreType.DMA((7,)),
+        ] + [
             shape for shape in (
                 pltpu.VMEM((coupled * GROUP, rows), F32),
                 pltpu.VMEM((2 * GROUP, rows), F32),
@@ -209,7 +225,7 @@
         ],
         compiler_params=pltpu.CompilerParams(vmem_limit_bytes=18 * 1024 * 1024),
         name="tile_sums",
-    )(order, groups, owner, channel, base, sky.reshape(tiles, coupled, rows), seen, keep, pairs, table)
+    )(order, groups, table, owner, channel, base, sky.reshape(tiles, coupled, rows), seen, keep, pairs)
 
 
 def eliminate(total, target, rho, full, directions):
@@ -282,13 +298,19 @@
     return jnp.where(lax.rem(i, 2) == 0, i // 2 + 1, nz - 1 - i // 2)
 
 
-def gather_kernel(nx, nz, bases, gains, base, table, order, groups, wide, mine,
+def gather_kernel(nx, nz, bases, far_gains, far_base, table, order, groups, gains, base, wide, mine, arrived,
                   z_recv, z_send, x_recv, x_send, c_recv, c_send):
     x, z, s = place()
     here, half = mine.shape[0], mine.shape[0] // 2
     stations = gains.shape[2]
+    fetched = [pltpu.make_async_copy(far_gains, gains, arrived.at[0]),
+               pltpu.make_async_copy(far_base, base, arrived.at[1])]
+    for copy in fetched:
+        copy.start()
     barrier, count = meet(x, z, s, nx, nz, False)
     wide[...] = jnp.zeros(wide.shape, F32)
+    for copy in fetched:
+        copy.wait()
     head = gains[...].astype(BF).astype(F32)
     wide[:, :, :stations] = head
     wide[:, :, HALF:HALF + stations] = gains[...] - head
@@ -312,34 +334,43 @@
         return carry
     lax.fori_loop(0, nz - 1, start_z, 0)
 
-    def x_copy(src, zz, d, e):
-        return sender(src, block(x, zz), x_send.at[e, d], x_recv.at[e, d], lax.rem(x + e, nx), z, s)
-    for e in range(1, nx):
-        x_copy(own, z, 0, e).start()
-    order[...], groups[...] = tile_order(base[...], bases, order.shape[1])
-
-    def pass_on(i, carry):
-        d = outward(i, nz)
-        zz = lax.rem(z + nz - d, nz)
-        sender(own, block(x, zz), z_send.at[d], z_recv.at[d], x, z, s).wait_recv()
-        for e in range(1, nx):
-            x_copy(block(x, zz), zz, d, e).start()
-        return carry
-    lax.fori_loop(0, nz - 1, pass_on, 0)
+    def x_copy(src, xx, zz, d, e, to):
+        return sender(src, block(xx, zz), x_send.at[e, d], x_recv.at[e, d], to, z, s)
+
+    def took_x(e, d):
+        xx, zz = lax.rem(x + nx - e, nx), lax.rem(z + nz - d, nz)
+        sender(own, block(xx, zz), x_send.at[e, d], x_recv.at[e, d], x, z, s).wait_recv()
+        return xx, zz
+    right, left = lax.rem(x + 1, nx), lax.rem(x + nx - 1, nx)
+    across = nx // 2
+    by_turns = [0] + [i // 2 + 1 if i % 2 == 0 else nz - 1 - i // 2 for i in range(nz - 1)]
+    lag = 3
+    for p in range(nz + lag):
+        if p < nz:
+            d = by_turns[p]
+            zz = lax.rem(z + nz - d, nz)
+            if d > 0:
+                sender(own, block(x, zz), z_send.at[d], z_recv.at[d], x, z, s).wait_recv()
+            src = own if d == 0 else block(x, zz)
+            x_copy(src, x, zz, d, 1, right).start()
+            x_copy(src, x, zz, d, nx - 1, left).start()
+            if d == 0:
+                order[...], groups[...] = tile_order(base[...], bases, order.shape[1])
+        if p >= lag:
+            d = by_turns[p - lag]
+            e, to = ((1, right), (nx - 1, left))[(p - lag) % 2]
+            xx, zz = took_x(e, d)
+            x_copy(block(xx, zz), xx, zz, d, across, to).start()
+            took_x(nx - e, d)
 
     def c_copy(e, h):
         xx = lax.rem(x + nx - e, nx)
         return sender(rows(xx, h), rows(xx, h), c_send.at[e], c_recv.at[e], x, z, 1 - s)
-    for e in (0, 1, 3, 2):
-        if e > 0:
-            xx = lax.rem(x + nx - e, nx)
-
-            def arrived(d, carry):
-                zz = lax.rem(z + nz - d, nz)
-                sender(own, block(xx, zz), x_send.at[e, d], x_recv.at[e, d], x, z, s).wait_recv()
-                return carry
-            lax.fori_loop(0, nz, arrived, 0)
+    for e in (0, 1, nx - 1):
         c_copy(e, s).start()
+    for d in by_turns:
+        took_x(across, d)
+    c_copy(across, s).start()
     for e in range(nx):
         c_copy(e, 1 - s).wait_recv()
 
@@ -347,11 +378,12 @@
         z_copy(d).wait_send()
         return carry
     lax.fori_loop(1, nz, done_z, 0)
-    for e in range(1, nx):
-        def done_x(d, carry):
-            x_copy(own, z, d, e).wait_send()
-            return carry
-        lax.fori_loop(0, nz, done_x, 0)
+
+    def done_x(d, carry):
+        for e in range(1, nx):
+            x_copy(own, x, z, d, e, x).wait_send()
+        return carry
+    lax.fori_loop(0, nz, done_x, 0)
     for e in range(nx):
         c_copy(e, s).wait_send()
 
@@ -365,9 +397,10 @@
         functools.partial(gather_kernel, nx, nz, bases),
         out_shape=(jax.ShapeDtypeStruct((nx * nz * here, rows, 2 * HALF), BF),
                    jax.ShapeDtypeStruct((1, slots), jnp.int32), jax.ShapeDtypeStruct((1, 128), jnp.int32)),
-        in_specs=[vmem, vmem],
+        in_specs=[pl.BlockSpec(memory_space=pltpu.HBM)] * 2,
         out_specs=(vmem, vmem, vmem),
-        scratch_shapes=[pltpu.VMEM((here, rows, 2 * HALF), F32), pltpu.VMEM((here, rows, 2 * HALF), BF),
+        scratch_shapes=[pltpu.VMEM(gains.shape, F32), pltpu.VMEM(base.shape, jnp.int32),
+                        pltpu.VMEM((here, rows, 2 * HALF), F32), pltpu.VMEM((here, rows, 2 * HALF), BF), dma((2,)),
                         dma((nz,)), dma((nz,)), dma((nx, nz)), dma((nx, nz)), dma((nx,)), dma((nx,))],
         compiler_params=pltpu.CompilerParams(collective_id=0, has_side_effects=True,
                                              vmem_limit_bytes=8 * 1024 * 1024),
@@ -388,7 +421,7 @@
 
 
 def finish_kernel(nx, nz, inverse, sums, gains, duals, cons, rho, gain_new, cons_new, dual_new,
-                  peer, two_out, two_in, x_out, x_in, z_out, z_in, own_z, total, full, wide,
+                  peer, two_out, two_in, x_out, x_in, z_out, z_in, z_sum, total, full, wide,
                   part_out, part_in, ring_in, last_in,
                   c_send, c_recv, t_send, t_recv, x_send, x_recv, z_send, z_recv,
                   p_send, p_recv, r_send, r_recv, l_send, l_recv):
@@ -411,6 +444,8 @@
     pl.semaphore_wait(barrier, count)
 
     def far(i):
+        if isinstance(i, int):
+            return (nz // 2 + (i + 1) // 2 * (1 if i % 2 == 0 else -1)) % nz
         step = (i + 1) // 2
         return lax.rem(jnp.where(lax.rem(i, 2) == 0, nz // 2 + step, nz // 2 + nz - step), nz)
 
@@ -432,9 +467,8 @@
         at = pl.ds(c * chunk + side * share, share)
         return sender(two_out.at[at], two_in.at[at], t_send.at[side, c], t_recv.at[side, c],
                       lax.rem(x + (right, left_)[side], nx), z, s)
-    c_copy(across, s).wait_recv()
-
-    def fill_two(c, carry):
+
+    def fill_two(c):
         def one(j, inner):
             i = c * chunk + j
             two_out[i] = packed(pair_sum(lax.rem(x + across, nx), lax.rem(z + far(i), nz)), plain)
@@ -442,17 +476,13 @@
         lax.fori_loop(0, chunk, one, 0)
         for side in range(2):
             t_copy(side, c).start()
-        return carry
-    lax.fori_loop(0, chunks, fill_two, 0)
 
     def x_copy(side, c):
         at = pl.ds(c * chunk, chunk)
         return sender(x_out.at[side, at], x_in.at[side, at], x_send.at[side, c], x_recv.at[side, c],
                       lax.rem(x + (right, left_)[side], nx), z, s)
-    c_copy(right, s).wait_recv()
-    c_copy(left_, s).wait_recv()
-
-    def fill_x(c, carry):
+
+    def fill_x(c):
         for side in range(2):
             t_copy(side, c).wait_recv()
             xx = lax.rem(x + (right, left_)[side], nx)
@@ -469,14 +499,23 @@
             lax.fori_loop(0, share, relayed, 0)
             lax.fori_loop(0, share, plainly, 0)
             x_copy(side, c).start()
-        return carry
-    lax.fori_loop(0, chunks, fill_x, 0)
-    c_copy(0, s).wait_recv()
+
+    quarter = nz // 4
+    n_far = 2 * quarter - 1
+    odd = lax.rem(z, 2)
+
+    def hop(i):
+        d = far(i)
+        if i >= n_far:
+            return d
+        if i == 0:
+            return quarter + 2 * quarter * odd
+        return d - quarter if i % 2 == 1 else d + quarter
 
     def z_copy(i):
-        return sender(z_out.at[i], z_in.at[i], z_send.at[i], z_recv.at[i], x, lax.rem(z + far(i), nz), s)
-
-    def fill_z(c, carry):
+        return sender(z_out.at[i], z_in.at[i], z_send.at[i], z_recv.at[i], x, lax.rem(z + hop(i), nz), s)
+
+    def fill_z(c):
         for side in range(2):
             x_copy(side, c).wait_recv()
 
@@ -486,22 +525,43 @@
             for side in range(2):
                 acc = acc + unpacked(x_in[side, i], plain)
             z_out[i] = packed(acc, plain)
-            own_z[...] = acc
-
-            @pl.when(i < nz - 1)
-            def _():
-                z_copy(i).start()
+            z_sum[i] = acc
             return inner
         lax.fori_loop(0, chunk, one, 0)
-        return carry
-    lax.fori_loop(0, chunks, fill_z, 0)
-    total[...] = own_z[...]
-
-    def take_z(i, carry):
+        for i in range(c * chunk, (c + 1) * chunk):
+            if i not in (n_far, n_far + 1, nz - 1):
+                z_copy(i).start()
+
+    def relay_z():
+        for i in range(n_far):
+            z_copy(i).wait_recv()
+            to = n_far + odd if i == 0 else n_far + (i + 1) % 2
+            z_sum[to] = z_sum[to] + unpacked(z_in[i], plain)
+        for i in (n_far, n_far + 1):
+            z_out[i] = packed(z_sum[i], plain)
+        for i in (n_far, n_far + 1):
+            z_copy(i).start()
+
+    c_copy(across, s).wait_recv()
+    for c in range(chunks - 1):
+        fill_two(c)
+    c_copy(right, s).wait_recv()
+    c_copy(left_, s).wait_recv()
+    fill_x(0)
+    fill_two(chunks - 1)
+    fill_x(1)
+    c_copy(0, s).wait_recv()
+    for c in range(chunks):
+        if c == chunks - 1:
+            relay_z()
+        fill_z(c)
+        if c + 2 < chunks:
+            fill_x(c + 2)
+    acc = z_sum[nz - 1]
+    for i in list(range(n_far + 2, nz - 1)) + [n_far, n_far + 1]:
         z_copy(i).wait_recv()
-        total[...] = total[...] + unpacked(z_in[i], plain)
-        return carry
-    lax.fori_loop(0, nz - 1, take_z, 0)
+        acc = acc + unpacked(z_in[i], plain)
+    total[...] = acc
 
     rho2 = jnp.concatenate([rho[...], rho[...]], axis=0)
     gain, dual = wide[0], wide[1]
@@ -589,18 +649,13 @@
     for e in range(nx):
         c_copy(e, 1 - s).wait_send()
 
-    def sent_x(c, carry):
+    for c in range(chunks):
         for side in range(2):
             t_copy(side, c).wait_send()
             x_copy(side, c).wait_send()
-        return carry
-    lax.fori_loop(0, chunks, sent_x, 0)
-
-    def sent_z(i, carry):
+    for i in range(nz - 1):
         z_copy(i).wait_send()
         r_copy(i + 1).wait_send()
-        return carry
-    lax.fori_loop(0, nz - 1, sent_z, 0)
     for e, f in near:
         p_copy(e, f).wait_send()
         l_copy(e, f, me).wait_send()
@@ -629,7 +684,7 @@
             pltpu.VMEM((2, nz, wire, lanes), BF),
             pltpu.VMEM((nz, wire, lanes), BF),
             pltpu.VMEM((nz, wire, lanes), BF),
-            pltpu.VMEM((terms, lanes), F32),
+            pltpu.VMEM((nz, terms, lanes), F32),
             pltpu.VMEM((terms, lanes), F32),
             pltpu.VMEM((2, rows * rows // 4, lanes), F32),
             pltpu.VMEM((2 + degrees, rows, lanes), F32),

time: 132 us -> 131 us (level)
    pallas_call x1, Pallas kernels: 51.7 us -> 48.2 us  [finish(): pl.pallas_call(functools.partial(finish_kernel, nx, nz, inverse), out_sha...]
    pallas_call x1, Pallas kernels: 44.9 us -> 48.3 us  [gather_gains(): pl.pallas_call(functools.partial(gather_kernel, nx, nz, bases), out_shape...]
where the time goes in v3:
time: 131 us; the launch traced here: 132 us
  Pallas kernels  121 us (92%)
  local copies, waits for them, and re-layouts  9.59 us (7%)
    pallas_call x1, Pallas kernels, gather_gains(): pl.pallas_call(functools.partial(gather_kernel, nx, nz, bases), out_shape...  48.3 us
    pallas_call x1, Pallas kernels, finish(): pl.pallas_call(functools.partial(finish_kernel, nx, nz, inverse), out_sha...  48.2 us
    pallas_call x1, Pallas kernels, tile_sums(): pl.pallas_call(functools.partial(tile_kernel, half_count), out_shape=jax....  24.8 us
    unnamed x29, local copies, waits for them, and re-layouts  9.52 us

profile of v3, /device:TPU:33, one launch (start us, length us, event | category | flops | bytes accessed | tf_op | source)
XLA Modules:
  0.0 131.6 jit_solution(1409808330311015068)
XLA Ops:
  0.6 0.0 copy-start.12
  0.6 0.0 copy-start.3
  0.7 0.8 copy-done.3
  1.4 0.0 copy-start.8
  1.4 0.7 copy-done.8
  2.1 48.3 %gather_gains.1 = (bf16[256,16,128]{2,1,0:T(8,128)(2,1)S(1)}, s32[1,768]{1,0:T(1,128)S(1)}, s32[1,128]{1,0:T(1,128)S(1)}) custom-call(f32[4,16,62]{2,1,0:T(8,128)S(1)} %bitcast.22, s32[1,512]{1,0:T(1,128)S(1)} %bitcast.29), custom_call_target="tpu_custom_call" | custom-call | tf_op jit(solution)/shard_map/gather_gains/pallas_call | solution.py:396
  50.4 0.0 copy-start
  50.4 1.6 %copy-done = bf16[512,8,2,128]{3,2,1,0:T(2,128)(2,1)S(1)} copy-done((bf16[512,8,2,128]{3,2,1,0:T(2,128)(2,1)S(1)}, bf16[512,8,2,128]{3,2,1,0:T(2,128)(2,1)}, u32[]{:S(2)}) %copy-start) | copy-done | bytes 2097176
  52.0 0.9 copy-done.1
  52.9 0.9 copy-done.2
  53.9 0.7 copy-done.7
  54.6 0.7 copy-done.9
  55.3 0.7 copy-done.10
  56.0 0.7 copy-done.11
  56.6 24.8 %tile_sums.1.sums = f32[129,80,128]{2,1,0:T(8,128)S(1)} custom-call(s32[1,768]{1,0:T(1,128)S(1)} %get-tuple-element.9.order, s32[1,128]{1,0:T(1,128)S(1)} %get-tuple-element.10.groups, bf16[256,16,128]{2,1,0:T(8,128)(2,1)S(1)} %get-tuple-element.11.table, s32[512]{0:T(512)S(1)} %bitcast.30, s32[512]{0:T(512)S(1)} %copy-done.11, s32[512]{0:T(512)S(1)} %copy-done.9, ...), custom_call_target="tpu_custom_call" | custom-call | tf_op jit(solution)/shard_map/tile_sums/pallas_call | solution.py:204
  81.5 0.0 copy-done.12
  81.5 0.1 broadcast_in_dim.2.rho
  81.6 0.0 copy-done.4
  81.6 0.0 copy-done.5
  81.6 0.0 copy-done.6
  81.6 48.2 %finish.1 = (f32[2,16,62]{2,1,0:T(8,128)S(1)}, f32[4,16,62]{2,1,0:T(8,128)S(1)}, f32[2,16,62]{2,1,0:T(8,128)S(1)}) custom-call(f32[129,80,128]{2,1,0:T(8,128)S(1)} %tile_sums.1.sums, f32[4,16,62]{2,1,0:T(8,128)S(1)} %bitcast.23, f32[2,16,62]{2,1,0:T(8,128)S(1)} %bitcast.26, f32[4,16,62]{2,1,0:T(8,128)S(1)} %bitcast.24, f32[8,128]{1,0:T(8,128)S(1)} %broadcast_in_dim.2.rho), custom_call_target="tpu_custom_call" | custom-call | tf_op jit(solution)/shard_map/finish/pallas_call | solution.py:673
  129.8 0.6 copy.17
  130.4 0.6 copy.18
  131.0 0.6 copy.19
  (9 shorter events, 0.0 us)
Async XLA Ops:
  0.6 80.9 %copy-start.12 = (f32[8]{0:T(128)S(1)}, f32[8]{0:T(128)}, u32[]{:S(2)}) copy-start(f32[8]{0:T(128)} %param.21) | copy-start | bytes 100
  0.6 0.8 copy-start.3
  1.4 0.7 copy-start.8
  2.1 79.5 %copy-start.4 = (f32[4,2,62,8]{2,3,1,0:T(8,128)S(1)}, f32[4,2,62,8]{2,3,1,0:T(8,128)}, u32[]{:S(2)}) copy-start(f32[4,2,62,8]{2,3,1,0:T(8,128)} %param.18) | copy-start | bytes 47620
  50.4 1.6 %copy-start = (bf16[512,8,2,128]{3,2,1,0:T(2,128)(2,1)S(1)}, bf16[512,8,2,128]{3,2,1,0:T(2,128)(2,1)}, u32[]{:S(2)}) copy-start(bf16[512,8,2,128]{3,2,1,0:T(2,128)(2,1)} %param.11) | copy-start | bytes 6291460
  52.0 0.9 copy-start.1
  52.9 0.9 copy-start.2
  53.9 0.7 copy-start.7
  54.6 0.7 copy-start.9
  55.3 0.7 copy-start.10
  56.0 0.7 copy-start.11
  56.6 24.9 %copy-start.5 = (f32[4,2,62,8]{2,3,1,0:T(8,128)S(1)}, f32[4,2,62,8]{2,3,1,0:T(8,128)}, u32[]{:S(2)}) copy-start(f32[4,2,62,8]{2,3,1,0:T(8,128)} %param.20) | copy-start | bytes 47620
  56.6 24.9 %copy-start.6 = (f32[2,2,62,8]{2,3,1,0:T(8,128)S(1)}, f32[2,2,62,8]{2,3,1,0:T(8,128)}, u32[]{:S(2)}) copy-start(f32[2,2,62,8]{2,3,1,0:T(8,128)} %param.19) | copy-start | bytes 23812

commit v4 on v2

--- a/solution.py
+++ b/solution.py
@@ -262,20 +262,21 @@
         device_id={XS: x, ZS: z, "sub": s}, device_id_type=pl.DeviceIdType.MESH)
 
 
-def meet(x, z, s, nx, nz, crossed):
+def meet(x, z, s, nx, nz, reach, crossed):
     barrier = pltpu.get_barrier_semaphore()
 
     def ring(d, carry):
         pl.semaphore_signal(barrier, inc=1, device_id={XS: x, ZS: lax.rem(z + d, nz), "sub": s},
                             device_id_type=pl.DeviceIdType.MESH)
         return carry
-    lax.fori_loop(1, nz, ring, 0)
+    lax.fori_loop(1, reach + 1, ring, 0)
+    lax.fori_loop(max(reach + 1, nz - reach), nz, ring, 0)
     near = [(e, f) for e in range(nx) for f in range(2) if e + f > 0 and (crossed or e * f == 0)]
     for e, f in near:
         pl.semaphore_signal(barrier, inc=1,
                             device_id={XS: lax.rem(x + e, nx), ZS: z, "sub": s + f - 2 * s * f},
                             device_id_type=pl.DeviceIdType.MESH)
-    return barrier, nz - 1 + len(near)
+    return barrier, min(nz - 1, 2 * reach) + len(near)
 
 
 def outward(i, nz):
@@ -287,7 +288,7 @@
     x, z, s = place()
     here, half = mine.shape[0], mine.shape[0] // 2
     stations = gains.shape[2]
-    barrier, count = meet(x, z, s, nx, nz, False)
+    barrier, count = meet(x, z, s, nx, nz, nz - 1, False)
     wide[...] = jnp.zeros(wide.shape, F32)
     head = gains[...].astype(BF).astype(F32)
     wide[:, :, :stations] = head
@@ -371,6 +372,7 @@
                         dma((nz,)), dma((nz,)), dma((nx, nz)), dma((nx, nz)), dma((nx,)), dma((nx,))],
         compiler_params=pltpu.CompilerParams(collective_id=0, has_side_effects=True,
                                              vmem_limit_bytes=8 * 1024 * 1024),
+        cost_estimate=pl.CostEstimate(flops=20000000000, bytes_accessed=20000000, transcendentals=0),
         name="gather_gains",
     )(gains, base)
 
@@ -388,10 +390,10 @@
 
 
 def finish_kernel(nx, nz, inverse, sums, gains, duals, cons, rho, gain_new, cons_new, dual_new,
-                  peer, two_out, two_in, x_out, x_in, z_out, z_in, own_z, total, full, wide,
+                  peer, two_out, two_in, x_out, x_in, z_out, z_in, z_sum, total, full, wide,
                   part_out, part_in, ring_in, last_in,
                   c_send, c_recv, t_send, t_recv, x_send, x_recv, z_send, z_recv,
-                  p_send, p_recv, r_send, r_recv, l_send, l_recv):
+                  p_send, p_recv, r_send, r_recv, l_send, l_recv, token):
     x, z, s = place()
     directions = rho.shape[0]
     degrees, _, stations = cons.shape
@@ -399,7 +401,7 @@
     plain = directions * directions
     chunk = 4
     nodes = nx * nz
-    barrier, count = meet(x, z, s, nx, nz, True)
+    barrier, count = meet(x, z, s, nx, nz, 1, True)
 
     wide[...] = jnp.zeros(wide.shape, F32)
     for h in range(half_count):
@@ -411,8 +413,21 @@
     pl.semaphore_wait(barrier, count)
 
     def far(i):
+        if isinstance(i, int):
+            return (nz // 2 + (i + 1) // 2 * (1 if i % 2 == 0 else -1)) % nz
         step = (i + 1) // 2
         return lax.rem(jnp.where(lax.rem(i, 2) == 0, nz // 2 + step, nz // 2 + nz - step), nz)
+
+    def tell():
+        for side in range(2):
+            pl.semaphore_signal(token.at[side], inc=1, device_id={XS: x, ZS: lax.rem(z + (1, nz - 1)[side], nz), "sub": s},
+                                device_id_type=pl.DeviceIdType.MESH)
+
+    def hear():
+        for side in range(2):
+            pl.semaphore_wait(token.at[side], 1)
+    n_tokens = nz // 2 - 1
+    tell()
 
     def c_copy(e, h):
         xx = lax.rem(x + e, nx)
@@ -432,9 +447,8 @@
         at = pl.ds(c * chunk + side * share, share)
         return sender(two_out.at[at], two_in.at[at], t_send.at[side, c], t_recv.at[side, c],
                       lax.rem(x + (right, left_)[side], nx), z, s)
-    c_copy(across, s).wait_recv()
-
-    def fill_two(c, carry):
+
+    def fill_two(c):
         def one(j, inner):
             i = c * chunk + j
             two_out[i] = packed(pair_sum(lax.rem(x + across, nx), lax.rem(z + far(i), nz)), plain)
@@ -442,17 +456,13 @@
         lax.fori_loop(0, chunk, one, 0)
         for side in range(2):
             t_copy(side, c).start()
-        return carry
-    lax.fori_loop(0, chunks, fill_two, 0)
 
     def x_copy(side, c):
         at = pl.ds(c * chunk, chunk)
         return sender(x_out.at[side, at], x_in.at[side, at], x_send.at[side, c], x_recv.at[side, c],
                       lax.rem(x + (right, left_)[side], nx), z, s)
-    c_copy(right, s).wait_recv()
-    c_copy(left_, s).wait_recv()
-
-    def fill_x(c, carry):
+
+    def fill_x(c):
         for side in range(2):
             t_copy(side, c).wait_recv()
             xx = lax.rem(x + (right, left_)[side], nx)
@@ -469,14 +479,23 @@
             lax.fori_loop(0, share, relayed, 0)
             lax.fori_loop(0, share, plainly, 0)
             x_copy(side, c).start()
-        return carry
-    lax.fori_loop(0, chunks, fill_x, 0)
-    c_copy(0, s).wait_recv()
+
+    quarter = nz // 4
+    n_far = 2 * quarter - 1
+    odd = lax.rem(z, 2)
+
+    def hop(i):
+        d = far(i)
+        if i >= n_far:
+            return d
+        if i == 0:
+            return quarter + 2 * quarter * odd
+        return d - quarter if i % 2 == 1 else d + quarter
 
     def z_copy(i):
-        return sender(z_out.at[i], z_in.at[i], z_send.at[i], z_recv.at[i], x, lax.rem(z + far(i), nz), s)
-
-    def fill_z(c, carry):
+        return sender(z_out.at[i], z_in.at[i], z_send.at[i], z_recv.at[i], x, lax.rem(z + hop(i), nz), s)
+
+    def fill_z(c):
         for side in range(2):
             x_copy(side, c).wait_recv()
 
@@ -486,22 +505,52 @@
             for side in range(2):
                 acc = acc + unpacked(x_in[side, i], plain)
             z_out[i] = packed(acc, plain)
-            own_z[...] = acc
-
-            @pl.when(i < nz - 1)
-            def _():
-                z_copy(i).start()
+            z_sum[i] = acc
             return inner
         lax.fori_loop(0, chunk, one, 0)
-        return carry
-    lax.fori_loop(0, chunks, fill_z, 0)
-    total[...] = own_z[...]
-
-    def take_z(i, carry):
+        for i in range(c * chunk, (c + 1) * chunk):
+            if i not in (n_far, n_far + 1, nz - 1):
+                z_copy(i).start()
+
+    def relay_z():
+        for i in range(n_far):
+            z_copy(i).wait_recv()
+            to = n_far + odd if i == 0 else n_far + (i + 1) % 2
+            z_sum[to] = z_sum[to] + unpacked(z_in[i], plain)
+        for i in (n_far, n_far + 1):
+            z_out[i] = packed(z_sum[i], plain)
+        for i in (n_far, n_far + 1):
+            z_copy(i).start()
+
+    c_copy(across, s).wait_recv()
+    hear()
+    tell()
+    for c in range(chunks - 1):
+        fill_two(c)
+    hear()
+    tell()
+    c_copy(right, s).wait_recv()
+    c_copy(left_, s).wait_recv()
+    fill_x(0)
+    hear()
+    tell()
+    fill_two(chunks - 1)
+    fill_x(1)
+    c_copy(0, s).wait_recv()
+    for c in range(chunks):
+        if c == chunks - 1:
+            relay_z()
+        fill_z(c)
+        if c + 2 < chunks:
+            fill_x(c + 2)
+        hear()
+        if c + 4 < n_tokens:
+            tell()
+    acc = z_sum[nz - 1]
+    for i in list(range(n_far + 2, nz - 1)) + [n_far, n_far + 1]:
         z_copy(i).wait_recv()
-        total[...] = total[...] + unpacked(z_in[i], plain)
-        return carry
-    lax.fori_loop(0, nz - 1, take_z, 0)
+        acc = acc + unpacked(z_in[i], plain)
+    total[...] = acc
 
     rho2 = jnp.concatenate([rho[...], rho[...]], axis=0)
     gain, dual = wide[0], wide[1]
@@ -589,18 +638,13 @@
     for e in range(nx):
         c_copy(e, 1 - s).wait_send()
 
-    def sent_x(c, carry):
+    for c in range(chunks):
         for side in range(2):
             t_copy(side, c).wait_send()
             x_copy(side, c).wait_send()
-        return carry
-    lax.fori_loop(0, chunks, sent_x, 0)
-
-    def sent_z(i, carry):
+    for i in range(nz - 1):
         z_copy(i).wait_send()
         r_copy(i + 1).wait_send()
-        return carry
-    lax.fori_loop(0, nz - 1, sent_z, 0)
     for e, f in near:
         p_copy(e, f).wait_send()
         l_copy(e, f, me).wait_send()
@@ -629,7 +673,7 @@
             pltpu.VMEM((2, nz, wire, lanes), BF),
             pltpu.VMEM((nz, wire, lanes), BF),
             pltpu.VMEM((nz, wire, lanes), BF),
-            pltpu.VMEM((terms, lanes), F32),
+            pltpu.VMEM((nz, terms, lanes), F32),
             pltpu.VMEM((terms, lanes), F32),
             pltpu.VMEM((2, rows * rows // 4, lanes), F32),
             pltpu.VMEM((2 + degrees, rows, lanes), F32),
@@ -640,6 +684,7 @@
             dma((nx,)), dma((nx,)), dma((2, chunks)), dma((2, chunks)), dma((2, chunks)), dma((2, chunks)),
             dma((nz,)), dma((nz,)),
             dma((pieces,)), dma((pieces,)), dma((nz,)), dma((nz,)), dma((pieces,)), dma((pieces,)),
+            pltpu.SemaphoreType.REGULAR((2,)),
         ],
         compiler_params=pltpu.CompilerParams(collective_id=1, has_side_effects=True,
                                              vmem_limit_bytes=18 * 1024 * 1024),

time: 132 us -> 117 us (0.89)
  Pallas kernels: 121 us -> 113 us
  local copies, waits for them, and re-layouts: 9.59 us -> 3.38 us
    pallas_call x1, Pallas kernels: 51.7 us -> 42.6 us  [finish(): pl.pallas_call(functools.partial(finish_kernel, nx, nz, inverse), out_sha...]
    unnamed x29, local copies, waits for them, and re-layouts: 9.52 us -> 3.31 us
where the time goes in v4:
time: 117 us
  Pallas kernels  113 us (97%)
  local copies, waits for them, and re-layouts  3.38 us (3%)
    pallas_call x1, Pallas kernels, gather_gains(): pl.pallas_call(functools.partial(gather_kernel, nx, nz, bases), out_shape...  45.4 us
    pallas_call x1, Pallas kernels, finish(): pl.pallas_call(functools.partial(finish_kernel, nx, nz, inverse), out_sha...  42.6 us
    pallas_call x1, Pallas kernels, tile_sums(): pl.pallas_call(functools.partial(tile_kernel, half_count), out_shape=jax....  24.6 us
    unnamed x29, local copies, waits for them, and re-layouts  3.31 us

profile of v4, /device:TPU:33, one launch (start us, length us, event | category | flops | bytes accessed | tf_op | source)
XLA Modules:
  0.0 116.8 jit_solution(14330169118210183974)
XLA Ops:
  0.6 0.0 copy-start.3
  0.6 0.7 copy-done.3
  1.4 0.7 copy-done.8
  2.1 0.0 copy-start.9
  2.1 0.0 copy-start.10
  2.1 45.4 %gather_gains.1 = (bf16[256,16,128]{2,1,0:T(8,128)(2,1)S(1)}, s32[1,768]{1,0:T(1,128)S(1)}, s32[1,128]{1,0:T(1,128)S(1)}) custom-call(f32[4,16,62]{2,1,0:T(8,128)S(1)} %bitcast.22, s32[1,512]{1,0:T(1,128)S(1)} %bitcast.29), custom_call_target="tpu_custom_call" | custom-call | flops 20000000000 | bytes 20000000 | tf_op jit(solution)/shard_map/gather_gains/pallas_call | solution.py:365
  47.5 0.0 copy-start.12
  47.5 0.0 copy-start.4
  47.5 0.0 copy-start.5
  47.6 0.0 copy-start.6
  47.6 0.0 copy-done
  47.6 0.0 copy-done.1
  47.6 0.0 copy-done.2
  47.6 0.0 copy-done.7
  47.6 0.0 copy-done.9
  47.6 0.0 copy-done.10
  47.6 0.0 copy-done.11
  47.6 24.6 %tile_sums.1.sums = f32[129,80,128]{2,1,0:T(8,128)S(1)} custom-call(s32[1,768]{1,0:T(1,128)S(1)} %get-tuple-element.9.order, s32[1,128]{1,0:T(1,128)S(1)} %get-tuple-element.10.groups, s32[512]{0:T(512)S(1)} %bitcast.30, s32[512]{0:T(512)S(1)} %copy-done.11, s32[512]{0:T(512)S(1)} %copy-done.9, bf16[512,16,128]{2,1,0:T(8,128)(2,1)S(1)} %bitcast.21, ...), custom_call_target="tpu_custom_call" | custom-call | tf_op jit(solution)/shard_map/tile_sums/pallas_call | solution.py:194
  72.3 0.1 broadcast_in_dim.2.rho
  72.3 0.0 copy-done.4
  72.4 42.6 %finish.1 = (f32[2,16,62]{2,1,0:T(8,128)S(1)}, f32[4,16,62]{2,1,0:T(8,128)S(1)}, f32[2,16,62]{2,1,0:T(8,128)S(1)}) custom-call(f32[129,80,128]{2,1,0:T(8,128)S(1)} %tile_sums.1.sums, f32[4,16,62]{2,1,0:T(8,128)S(1)} %bitcast.23, f32[2,16,62]{2,1,0:T(8,128)S(1)} %bitcast.26, f32[4,16,62]{2,1,0:T(8,128)S(1)} %bitcast.24, f32[8,128]{1,0:T(8,128)S(1)} %broadcast_in_dim.2.rho), custom_call_target="tpu_custom_call" | custom-call | tf_op jit(solution)/shard_map/finish/pallas_call | solution.py:662
  114.9 0.6 copy.17
  115.5 0.6 copy.18
  116.2 0.6 copy.19
  (9 shorter events, 0.0 us)
Async XLA Ops:
  0.6 0.8 copy-start.3
  1.4 0.7 copy-start.8
  2.1 45.5 %copy-start = (bf16[512,8,2,128]{3,2,1,0:T(2,128)(2,1)S(1)}, bf16[512,8,2,128]{3,2,1,0:T(2,128)(2,1)}, u32[]{:S(2)}) copy-start(bf16[512,8,2,128]{3,2,1,0:T(2,128)(2,1)} %param.11) | copy-start | bytes 6291460
  2.1 45.5 %copy-start.1 = (bf16[512,2,128]{2,1,0:T(2,128)(2,1)S(1)}, bf16[512,2,128]{2,1,0:T(2,128)(2,1)}, u32[]{:S(2)}) copy-start(bf16[512,2,128]{2,1,0:T(2,128)(2,1)} %seen.1) | copy-start | bytes 786436
  2.1 45.5 %copy-start.2 = (s32[512,128]{1,0:T(8,128)S(1)}, s32[512,128]{1,0:T(8,128)}, u32[]{:S(2)}) copy-start(s32[512,128]{1,0:T(8,128)} %keep.1) | copy-start | bytes 786436
  2.1 45.5 %copy-start.7 = (s32[15,2,128]{2,1,0:T(2,128)S(1)}, s32[15,2,128]{2,1,0:T(2,128)}, u32[]{:S(2)}) copy-start(s32[15,2,128]{2,1,0:T(2,128)} %pairs.1) | copy-start | bytes 46084
  2.1 45.5 %copy-start.9 = (s32[512]{0:T(512)S(1)}, s32[512]{0:T(512)}, u32[]{:S(2)}) copy-start(s32[512]{0:T(512)} %base.1) | copy-start | bytes 6148
  2.1 45.5 %copy-start.10 = (s32[512,1]{0,1:T(1,128)S(1)}, s32[512,1]{0,1:T(1,128)}, u32[]{:S(2)}) copy-start(s32[512,1]{0,1:T(1,128)} %param.14) | copy-start | bytes 6148
  2.1 45.5 %copy-start.11 = (s32[512]{0:T(512)S(1)}, s32[512]{0:T(512)}, u32[]{:S(2)}) copy-start(s32[512]{0:T(512)} %channel.1) | copy-start | bytes 6148
  47.5 24.8 %copy-start.12 = (f32[8]{0:T(128)S(1)}, f32[8]{0:T(128)}, u32[]{:S(2)}) copy-start(f32[8]{0:T(128)} %param.21) | copy-start | bytes 100
  47.5 24.8 %copy-start.4 = (f32[4,2,62,8]{2,3,1,0:T(8,128)S(1)}, f32[4,2,62,8]{2,3,1,0:T(8,128)}, u32[]{:S(2)}) copy-start(f32[4,2,62,8]{2,3,1,0:T(8,128)} %param.18) | copy-start | bytes 47620
  47.5 24.8 %copy-start.5 = (f32[4,2,62,8]{2,3,1,0:T(8,128)S(1)}, f32[4,2,62,8]{2,3,1,0:T(8,128)}, u32[]{:S(2)}) copy-start(f32[4,2,62,8]{2,3,1,0:T(8,128)} %param.20) | copy-start | bytes 47620
  47.6 24.8 %copy-start.6 = (f32[2,2,62,8]{2,3,1,0:T(8,128)S(1)}, f32[2,2,62,8]{2,3,1,0:T(8,128)}, u32[]{:S(2)}) copy-start(f32[2,2,62,8]{2,3,1,0:T(8,128)} %param.19) | copy-start | bytes 23812

commit v5 on v4

--- a/solution.py
+++ b/solution.py
@@ -98,43 +98,34 @@
         for t in range(GROUP):
             named = order[0, g * GROUP + t]
             tile = jnp.where(named < tiles, named, 0)
-            sky_s[pl.ds(t, coupled, stride=GROUP), :] = sky[tile].astype(F32)
-            seen_s[pl.ds(t, 2, stride=GROUP), :] = seen[tile].astype(F32)
-            keep_s[pl.ds(t, 1), :] = keep[pl.ds(tile, 1), :]
+            kept = keep[pl.ds(tile, 1), :] > 0
+            sky_s[pl.ds(t, coupled, stride=GROUP), :] = jnp.where(kept, sky[tile].astype(F32), 0.0)
+            seen_s[pl.ds(t, 2, stride=GROUP), :] = jnp.where(kept, seen[tile].astype(F32), 0.0)
             gain_s[pl.ds(t, coupled, stride=GROUP), :] = table[owner[tile] * channels_here + channel[tile]].astype(F32)
         near_far[...] = jnp.dot(gain_s[...].astype(BF), chosen(g)[...], preferred_element_type=F32)
 
     def products(of):
         sky_s, seen_s, keep_s, _, near_far, terms, _ = buffers[of]
-        kept = keep_s[...] > 0
-
         def block(ref, i):
             return ref[i * GROUP:(i + 1) * GROUP, :]
 
-        res_r = jnp.where(kept, block(seen_s, 0), 0.0)
-        res_i = jnp.where(kept, block(seen_s, 1), 0.0)
-        a_r, a_i, b_r, b_i = [], [], [], []
-        mod_r = mod_i = None
+        res_r = block(seen_s, 0)
+        res_i = block(seen_s, 1)
+        v_r, v_i = [], []
         for k in range(directions):
-            c_r = jnp.where(kept, block(sky_s, 2 * k), 0.0)
-            c_i = jnp.where(kept, block(sky_s, 2 * k + 1), 0.0)
+            c_r = block(sky_s, 2 * k)
+            c_i = block(sky_s, 2 * k + 1)
             p_r, p_i = (block(near_far, c * directions + k)[:, :rows] for c in range(2))
             q_r, q_i = (block(near_far, c * directions + k)[:, rows:] for c in range(2))
             x_r = c_r * q_r + c_i * q_i
             x_i = c_i * q_r - c_r * q_i
-            a_r.append(x_r)
-            a_i.append(x_i)
-            b_r.append(c_r * p_r - c_i * p_i)
-            b_i.append(-(c_r * p_i + c_i * p_r))
-            m_r = p_r * x_r - p_i * x_i
-            m_i = p_r * x_i + p_i * x_r
-            mod_r = m_r if mod_r is None else mod_r + m_r
-            mod_i = m_i if mod_i is None else mod_i + m_i
-        res_r = res_r - mod_r
-        res_i = res_i - mod_i
-
-        for side, (v_r, v_i, w_r, w_i) in enumerate(
-                ((a_r, a_i, res_r, res_i), (b_r, b_i, res_r, -res_i))):
+            v_r.append(x_r)
+            v_i.append(x_i)
+            res_r = res_r - (p_r * x_r - p_i * x_i)
+            res_i = res_i - (p_r * x_i + p_i * x_r)
+        w_r, w_i = res_r, res_i
+
+        for side in range(2):
             pending = {}
 
             def put(j, value):
@@ -144,6 +135,14 @@
                     both = jnp.concatenate([pending.pop(lo), pending.pop(lo + 1)], axis=0)
                     terms[lo * GROUP:(lo + 2) * GROUP, side * rows:(side + 1) * rows] = both.astype(BF)
 
+            if side == 1:
+                v_r, v_i, w_i = [], [], -res_i
+                for k in range(directions):
+                    c_r = block(sky_s, 2 * k)
+                    c_i = block(sky_s, 2 * k + 1)
+                    p_r, p_i = (block(near_far, c * directions + k)[:, :rows] for c in range(2))
+                    v_r.append(c_r * p_r - c_i * p_i)
+                    v_i.append(-(c_r * p_i + c_i * p_r))
             for (k, m), j in real.items():
                 put(j, v_r[k] * v_r[m] + v_i[k] * v_i[m])
             for (k, m), j in imag.items():
@@ -309,7 +308,7 @@
         return sender(own, block(x, z), z_send.at[d], z_recv.at[d], x, lax.rem(z + d, nz), s)
 
     def start_z(i, carry):
-        z_copy(outward(i, nz)).start()
+        z_copy(outward(nz - 2 - i, nz)).start()
         return carry
     lax.fori_loop(0, nz - 1, start_z, 0)
 
@@ -323,7 +322,7 @@
         d = outward(i, nz)
         zz = lax.rem(z + nz - d, nz)
         sender(own, block(x, zz), z_send.at[d], z_recv.at[d], x, z, s).wait_recv()
-        for e in range(1, nx):
+        for e in (nx // 2, 1, nx - 1):
             x_copy(block(x, zz), zz, d, e).start()
         return carry
     lax.fori_loop(0, nz - 1, pass_on, 0)
@@ -389,7 +388,7 @@
     return jnp.concatenate([v[:plain], v[plain:mid] + v[mid:]], axis=0)
 
 
-def finish_kernel(nx, nz, inverse, sums, gains, duals, cons, rho, gain_new, cons_new, dual_new,
+def finish_kernel(nx, nz, inverse, sums, gains, duals, cons, rho, result,
                   peer, two_out, two_in, x_out, x_in, z_out, z_in, z_sum, total, full, wide,
                   part_out, part_in, ring_in, last_in,
                   c_send, c_recv, t_send, t_recv, x_send, x_recv, z_send, z_recv,
@@ -398,6 +397,8 @@
     directions = rho.shape[0]
     degrees, _, stations = cons.shape
     half_count = duals.shape[0]
+    gain_new, dual_new = result.at[:half_count], result.at[half_count:2 * half_count]
+    cons_new = result.at[2 * half_count:]
     plain = directions * directions
     chunk = 4
     nodes = nx * nz
@@ -661,10 +662,9 @@
     chunks = nz // 4
     return pl.pallas_call(
         functools.partial(finish_kernel, nx, nz, inverse),
-        out_shape=(jax.ShapeDtypeStruct(duals.shape, F32), jax.ShapeDtypeStruct(cons.shape, F32),
-                   jax.ShapeDtypeStruct(duals.shape, F32)),
+        out_shape=jax.ShapeDtypeStruct((2 * duals.shape[0] + cons.shape[0],) + cons.shape[1:], F32),
         in_specs=[vmem] * 5,
-        out_specs=(vmem, vmem, vmem),
+        out_specs=vmem,
         scratch_shapes=[
             pltpu.VMEM((nx * nz, terms, lanes), F32),
             pltpu.VMEM((nz, wire, lanes), BF),
@@ -712,9 +712,10 @@
     sums = tile_sums(sky, seen, keep, order, groups, tile_owner[:, 0], tile_channel, tile_base, pairs, table,
                      nx * nz * sub_count, half_count)
     rho_rows = jnp.broadcast_to(rho[:, None], (directions, 2 * HALF))
-    gain_new, cons_new, dual_new = finish(sums, gain_rows, to_rows(duals), to_rows(consensus), rho_rows,
+    result = finish(sums, gain_rows, to_rows(duals), to_rows(consensus), rho_rows,
                                           gram_inverse(channels_here * nx * nz).tolist(), nx, nz)
-    return from_rows(gain_new), from_rows(cons_new), from_rows(dual_new)
+    return (from_rows(result[:half_count]), from_rows(result[2 * half_count:]),
+            from_rows(result[half_count:2 * half_count]))
 
 
 def solution(mesh):

time: 117 us -> 117 us (level)
    pallas_call x1, Pallas kernels: 42.6 us -> 44.7 us  [finish(): pl.pallas_call(functools.partial(finish_kernel, nx, nz, inverse), out_sha...]
    unnamed x29 -> x26, local copies, waits for them, and re-layouts: 3.31 us -> 1.49 us
    pallas_call x1, Pallas kernels: 45.4 us -> 44.1 us  [gather_gains(): pl.pallas_call(functools.partial(gather_kernel, nx, nz, bases), out_shape...]
    transpose x0 -> x2, local copies, waits for them, and re-layouts: none -> 1.23 us  [from_rows(): return jnp.transpose(x.reshape(n, 2, rows // 2, s), (0, 1, 3, 2))]
where the time goes in v5:
time: 117 us
  Pallas kernels  113 us (97%)
  local copies, waits for them, and re-layouts  2.79 us (2%)
    pallas_call x1, Pallas kernels, finish(): pl.pallas_call(functools.partial(finish_kernel, nx, nz, inverse), out_sha...  44.7 us
    pallas_call x1, Pallas kernels, gather_gains(): pl.pallas_call(functools.partial(gather_kernel, nx, nz, bases), out_shape...  44.1 us
    pallas_call x1, Pallas kernels, tile_sums(): pl.pallas_call(functools.partial(tile_kernel, half_count), out_shape=jax....  24.4 us

profile of v5, /device:TPU:33, one launch (start us, length us, event | category | flops | bytes accessed | tf_op | source)
XLA Modules:
  0.0 116.7 jit_solution(5797706206945315472)
XLA Ops:
  0.6 0.0 copy-start.3
  0.6 0.7 copy-done.3
  1.4 0.7 copy-done.8
  2.1 0.0 copy-start.9
  2.1 0.0 copy-start.10
  2.1 0.0 copy-start.11
  2.1 44.1 %gather_gains.1 = (bf16[256,16,128]{2,1,0:T(8,128)(2,1)S(1)}, s32[1,768]{1,0:T(1,128)S(1)}, s32[1,128]{1,0:T(1,128)S(1)}) custom-call(f32[4,16,62]{2,1,0:T(8,128)S(1)} %bitcast.25, s32[1,512]{1,0:T(1,128)S(1)} %bitcast.29), custom_call_target="tpu_custom_call" | custom-call | flops 20000000000 | bytes 20000000 | tf_op jit(solution)/shard_map/gather_gains/pallas_call | solution.py:364
  46.2 0.0 copy-start.12
  46.2 0.0 copy-start.4
  46.2 0.0 copy-start.5
  46.2 0.0 copy-start.6
  46.3 0.0 copy-done
  46.3 0.0 copy-done.1
  46.3 0.0 copy-done.2
  46.3 0.0 copy-done.7
  46.3 0.0 copy-done.9
  46.3 0.0 copy-done.10
  46.3 24.4 %tile_sums.1.sums = f32[129,80,128]{2,1,0:T(8,128)S(1)} custom-call(s32[1,768]{1,0:T(1,128)S(1)} %get-tuple-element.6.order, s32[1,128]{1,0:T(1,128)S(1)} %get-tuple-element.7.groups, s32[512]{0:T(512)S(1)} %bitcast.30, s32[512]{0:T(512)S(1)} %copy-done.11, s32[512]{0:T(512)S(1)} %copy-done.9, bf16[512,16,128]{2,1,0:T(8,128)(2,1)S(1)} %bitcast.24, ...), custom_call_target="tpu_custom_call" | custom-call | tf_op jit(solution)/shard_map/tile_sums/pallas_call | solution.py:193
  70.7 0.0 copy-done.12
  70.7 0.1 broadcast_in_dim.2.rho
  70.8 0.0 copy-done.5
  70.8 44.7 %finish.1 = f32[8,16,62]{2,1,0:T(8,128)S(1)} custom-call(f32[129,80,128]{2,1,0:T(8,128)S(1)} %tile_sums.1.sums, f32[4,16,62]{2,1,0:T(8,128)S(1)} %bitcast.26, f32[2,16,62]{2,1,0:T(8,128)S(1)} %bitcast.28, f32[4,16,62]{2,1,0:T(8,128)S(1)} %bitcast.27, f32[8,128]{1,0:T(8,128)S(1)} %broadcast_in_dim.2.rho), custom_call_target="tpu_custom_call" | custom-call | tf_op jit(solution)/shard_map/finish/pallas_call | solution.py:663
  115.5 0.6 slice_bitcast_fusion.1
  116.1 0.6 slice_bitcast_fusion
  (8 shorter events, 0.0 us)
Async XLA Ops:
  0.6 0.8 copy-start.3
  1.4 0.7 copy-start.8
  2.1 44.2 %copy-start = (bf16[512,8,2,128]{3,2,1,0:T(2,128)(2,1)S(1)}, bf16[512,8,2,128]{3,2,1,0:T(2,128)(2,1)}, u32[]{:S(2)}) copy-start(bf16[512,8,2,128]{3,2,1,0:T(2,128)(2,1)} %param.11) | copy-start | bytes 6291460
  2.1 44.2 %copy-start.1 = (bf16[512,2,128]{2,1,0:T(2,128)(2,1)S(1)}, bf16[512,2,128]{2,1,0:T(2,128)(2,1)}, u32[]{:S(2)}) copy-start(bf16[512,2,128]{2,1,0:T(2,128)(2,1)} %seen.1) | copy-start | bytes 786436
  2.1 44.2 %copy-start.2 = (s32[512,128]{1,0:T(8,128)S(1)}, s32[512,128]{1,0:T(8,128)}, u32[]{:S(2)}) copy-start(s32[512,128]{1,0:T(8,128)} %keep.1) | copy-start | bytes 786436
  2.1 44.2 %copy-start.7 = (s32[15,2,128]{2,1,0:T(2,128)S(1)}, s32[15,2,128]{2,1,0:T(2,128)}, u32[]{:S(2)}) copy-start(s32[15,2,128]{2,1,0:T(2,128)} %pairs.1) | copy-start | bytes 46084
  2.1 44.2 %copy-start.9 = (s32[512]{0:T(512)S(1)}, s32[512]{0:T(512)}, u32[]{:S(2)}) copy-start(s32[512]{0:T(512)} %base.1) | copy-start | bytes 6148
  2.1 44.2 %copy-start.10 = (s32[512,1]{0,1:T(1,128)S(1)}, s32[512,1]{0,1:T(1,128)}, u32[]{:S(2)}) copy-start(s32[512,1]{0,1:T(1,128)} %param.14) | copy-start | bytes 6148
  2.1 44.2 %copy-start.11 = (s32[512]{0:T(512)S(1)}, s32[512]{0:T(512)}, u32[]{:S(2)}) copy-start(s32[512]{0:T(512)} %channel.1) | copy-start | bytes 6148
  46.2 24.5 %copy-start.12 = (f32[8]{0:T(128)S(1)}, f32[8]{0:T(128)}, u32[]{:S(2)}) copy-start(f32[8]{0:T(128)} %param.21) | copy-start | bytes 100
  46.2 24.6 %copy-start.4 = (f32[4,2,62,8]{2,3,1,0:T(8,128)S(1)}, f32[4,2,62,8]{2,3,1,0:T(8,128)}, u32[]{:S(2)}) copy-start(f32[4,2,62,8]{2,3,1,0:T(8,128)} %param.18) | copy-start | bytes 47620
  46.2 24.5 %copy-start.5 = (f32[4,2,62,8]{2,3,1,0:T(8,128)S(1)}, f32[4,2,62,8]{2,3,1,0:T(8,128)}, u32[]{:S(2)}) copy-start(f32[4,2,62,8]{2,3,1,0:T(8,128)} %param.20) | copy-start | bytes 47620
  46.2 24.5 %copy-start.6 = (f32[2,2,62,8]{2,3,1,0:T(8,128)S(1)}, f32[2,2,62,8]{2,3,1,0:T(8,128)}, u32[]{:S(2)}) copy-start(f32[2,2,62,8]{2,3,1,0:T(8,128)} %param.19) | copy-start | bytes 23812

commit v6 on v5

--- a/solution.py
+++ b/solution.py
@@ -454,7 +454,7 @@
             i = c * chunk + j
             two_out[i] = packed(pair_sum(lax.rem(x + across, nx), lax.rem(z + far(i), nz)), plain)
             return inner
-        lax.fori_loop(0, chunk, one, 0)
+        lax.fori_loop(0, chunk, one, 0, unroll=True)
         for side in range(2):
             t_copy(side, c).start()
 
@@ -465,7 +465,6 @@
 
     def fill_x(c):
         for side in range(2):
-            t_copy(side, c).wait_recv()
             xx = lax.rem(x + (right, left_)[side], nx)
 
             def relayed(j, inner):
@@ -477,8 +476,9 @@
                 i = c * chunk + (1 - side) * share + j
                 x_out[side, i] = packed(pair_sum(xx, lax.rem(z + far(i), nz)), plain)
                 return inner
-            lax.fori_loop(0, share, relayed, 0)
-            lax.fori_loop(0, share, plainly, 0)
+            lax.fori_loop(0, share, plainly, 0, unroll=True)
+            t_copy(side, c).wait_recv()
+            lax.fori_loop(0, share, relayed, 0, unroll=True)
             x_copy(side, c).start()
 
     quarter = nz // 4
@@ -508,7 +508,7 @@
             z_out[i] = packed(acc, plain)
             z_sum[i] = acc
             return inner
-        lax.fori_loop(0, chunk, one, 0)
+        lax.fori_loop(0, chunk, one, 0, unroll=True)
         for i in range(c * chunk, (c + 1) * chunk):
             if i not in (n_far, n_far + 1, nz - 1):
                 z_copy(i).start()

time: 117 us -> 116 us (level)
  no operation moved by 1% of the time
where the time goes in v6:
time: 116 us
  Pallas kernels  113 us (97%)
  local copies, waits for them, and re-layouts  2.79 us (2%)
    pallas_call x1, Pallas kernels, finish(): pl.pallas_call(functools.partial(finish_kernel, nx, nz, inverse), out_sha...  44.1 us
    pallas_call x1, Pallas kernels, gather_gains(): pl.pallas_call(functools.partial(gather_kernel, nx, nz, bases), out_shape...  44.1 us
    pallas_call x1, Pallas kernels, tile_sums(): pl.pallas_call(functools.partial(tile_kernel, half_count), out_shape=jax....  24.3 us

profile of v6, /device:TPU:33, one launch (start us, length us, event | category | flops | bytes accessed | tf_op | source)
XLA Modules:
  0.0 116.1 jit_solution(6769105552409590761)
XLA Ops:
  0.6 0.0 copy-start.3
  0.6 0.7 copy-done.3
  1.4 0.7 copy-done.8
  2.1 0.0 copy-start.9
  2.1 0.0 copy-start.10
  2.1 0.0 copy-start.11
  2.1 44.1 %gather_gains.1 = (bf16[256,16,128]{2,1,0:T(8,128)(2,1)S(1)}, s32[1,768]{1,0:T(1,128)S(1)}, s32[1,128]{1,0:T(1,128)S(1)}) custom-call(f32[4,16,62]{2,1,0:T(8,128)S(1)} %bitcast.25, s32[1,512]{1,0:T(1,128)S(1)} %bitcast.29), custom_call_target="tpu_custom_call" | custom-call | flops 20000000000 | bytes 20000000 | tf_op jit(solution)/shard_map/gather_gains/pallas_call | solution.py:364
  46.2 0.0 copy-start.12
  46.2 0.0 copy-start.4
  46.2 0.0 copy-start.5
  46.2 0.0 copy-start.6
  46.3 0.0 copy-done
  46.3 0.0 copy-done.1
  46.3 0.0 copy-done.2
  46.3 0.0 copy-done.7
  46.3 0.0 copy-done.9
  46.3 0.0 copy-done.10
  46.3 24.3 %tile_sums.1.sums = f32[129,80,128]{2,1,0:T(8,128)S(1)} custom-call(s32[1,768]{1,0:T(1,128)S(1)} %get-tuple-element.6.order, s32[1,128]{1,0:T(1,128)S(1)} %get-tuple-element.7.groups, s32[512]{0:T(512)S(1)} %bitcast.30, s32[512]{0:T(512)S(1)} %copy-done.11, s32[512]{0:T(512)S(1)} %copy-done.9, bf16[512,16,128]{2,1,0:T(8,128)(2,1)S(1)} %bitcast.24, ...), custom_call_target="tpu_custom_call" | custom-call | tf_op jit(solution)/shard_map/tile_sums/pallas_call | solution.py:193
  70.7 0.0 copy-done.12
  70.7 0.1 broadcast_in_dim.2.rho
  70.8 0.0 copy-done.5
  70.8 44.1 %finish.1 = f32[8,16,62]{2,1,0:T(8,128)S(1)} custom-call(f32[129,80,128]{2,1,0:T(8,128)S(1)} %tile_sums.1.sums, f32[4,16,62]{2,1,0:T(8,128)S(1)} %bitcast.26, f32[2,16,62]{2,1,0:T(8,128)S(1)} %bitcast.28, f32[4,16,62]{2,1,0:T(8,128)S(1)} %bitcast.27, f32[8,128]{1,0:T(8,128)S(1)} %broadcast_in_dim.2.rho), custom_call_target="tpu_custom_call" | custom-call | tf_op jit(solution)/shard_map/finish/pallas_call | solution.py:663
  114.9 0.6 slice_bitcast_fusion.1
  115.5 0.6 slice_bitcast_fusion
  (8 shorter events, 0.0 us)
Async XLA Ops:
  0.6 0.8 copy-start.3
  1.4 0.7 copy-start.8
  2.1 44.2 %copy-start = (bf16[512,8,2,128]{3,2,1,0:T(2,128)(2,1)S(1)}, bf16[512,8,2,128]{3,2,1,0:T(2,128)(2,1)}, u32[]{:S(2)}) copy-start(bf16[512,8,2,128]{3,2,1,0:T(2,128)(2,1)} %param.11) | copy-start | bytes 6291460
  2.1 44.2 %copy-start.1 = (bf16[512,2,128]{2,1,0:T(2,128)(2,1)S(1)}, bf16[512,2,128]{2,1,0:T(2,128)(2,1)}, u32[]{:S(2)}) copy-start(bf16[512,2,128]{2,1,0:T(2,128)(2,1)} %seen.1) | copy-start | bytes 786436
  2.1 44.2 %copy-start.2 = (s32[512,128]{1,0:T(8,128)S(1)}, s32[512,128]{1,0:T(8,128)}, u32[]{:S(2)}) copy-start(s32[512,128]{1,0:T(8,128)} %keep.1) | copy-start | bytes 786436
  2.1 44.2 %copy-start.7 = (s32[15,2,128]{2,1,0:T(2,128)S(1)}, s32[15,2,128]{2,1,0:T(2,128)}, u32[]{:S(2)}) copy-start(s32[15,2,128]{2,1,0:T(2,128)} %pairs.1) | copy-start | bytes 46084
  2.1 44.2 %copy-start.9 = (s32[512]{0:T(512)S(1)}, s32[512]{0:T(512)}, u32[]{:S(2)}) copy-start(s32[512]{0:T(512)} %base.1) | copy-start | bytes 6148
  2.1 44.2 %copy-start.10 = (s32[512,1]{0,1:T(1,128)S(1)}, s32[512,1]{0,1:T(1,128)}, u32[]{:S(2)}) copy-start(s32[512,1]{0,1:T(1,128)} %param.14) | copy-start | bytes 6148
  2.1 44.2 %copy-start.11 = (s32[512]{0:T(512)S(1)}, s32[512]{0:T(512)}, u32[]{:S(2)}) copy-start(s32[512]{0:T(512)} %channel.1) | copy-start | bytes 6148
  46.2 24.5 %copy-start.12 = (f32[8]{0:T(128)S(1)}, f32[8]{0:T(128)}, u32[]{:S(2)}) copy-start(f32[8]{0:T(128)} %param.21) | copy-start | bytes 100
  46.2 24.5 %copy-start.4 = (f32[4,2,62,8]{2,3,1,0:T(8,128)S(1)}, f32[4,2,62,8]{2,3,1,0:T(8,128)}, u32[]{:S(2)}) copy-start(f32[4,2,62,8]{2,3,1,0:T(8,128)} %param.18) | copy-start | bytes 47620
  46.2 24.5 %copy-start.5 = (f32[4,2,62,8]{2,3,1,0:T(8,128)S(1)}, f32[4,2,62,8]{2,3,1,0:T(8,128)}, u32[]{:S(2)}) copy-start(f32[4,2,62,8]{2,3,1,0:T(8,128)} %param.20) | copy-start | bytes 47620
  46.2 24.5 %copy-start.6 = (f32[2,2,62,8]{2,3,1,0:T(8,128)S(1)}, f32[2,2,62,8]{2,3,1,0:T(8,128)}, u32[]{:S(2)}) copy-start(f32[2,2,62,8]{2,3,1,0:T(8,128)} %param.19) | copy-start | bytes 23812
